TPU v7x, 512 devices: a 4x2x32 block of a 4x8x32 slice. The times are simulated.
512 devices in a mesh: clip: 2 (over y), outer: 32 (over z), inner: 4 (over x), head: 2 (over core).
Axes of the slice: x: 4, y: 2, z: 32, core: 2. Of those that a mesh axis runs over, the one named last changes fastest.
The devices are a block of a 4x8x32 slice.
Arguments:
- tokens: bfloat16 [2, 4096, 3072], P('clip', ('outer', 'inner', 'head')), parts along dimension 0, may hold values from -6 to 6
- shift_mod: float32 [2, 3072], P('clip'), parts along dimension 0, may hold values from -3 to 3
- scale_mod: float32 [2, 3072], P('clip'), parts along dimension 0, may hold values from -1.5 to 1.5
- gate_mod: float32 [2, 3072], P('clip'), parts along dimension 0, may hold values from 0.5 to 2
- query_weight: bfloat16 [3072, 3072], P('outer', ('inner', 'head')), may hold values from -0.109375 to 0.109375
- key_weight: bfloat16 [3072, 3072], P('outer', ('inner', 'head')), may hold values from -0.109375 to 0.109375
- value_weight: bfloat16 [3072, 3072], P('outer', ('inner', 'head')), may hold values from -0.109375 to 0.109375
- out_weight: bfloat16 [3072, 3072], P(('inner', 'head'), 'outer'), may hold values from -0.109375 to 0.109375
- query_gain: float32 [128], replicated, may hold values from 1 to 18, as said below
- key_gain: float32 [128], replicated, may hold values from 1 to 18, as said below
Outputs:
- attended: bfloat16 [2, 4096, 3072], P('clip', ('outer', 'inner', 'head')), parts along dimension 0
There are 2 independent parts, one for each index of `clip`. A program takes and returns all parts, laid end to end along the dimension named above; an argument that names none is the same for every part. Nothing has to cross between parts.
Inputs may be any that keep to these rules, and one draw needn't show every extreme that they name: `query_gain`: 128 positive scales. `key_gain`: 128 positive scales.
All inputs are finite; a program needn't handle non-finite values.
Results may differ from a plain program's by a relative error of at most 0.015.
The roundings to bfloat16 on the way count: a program that leaves them out, or rounds other values in their place, can miss the bound.
Values may be sent and summed in bfloat16 or wider, within the bound.
No kernel may reach another device: no remote copies, remote signals or barrier semaphores. Data moves between devices by JAX's collectives and lax.ppermute only.
A program may use at most 64 MiB of HBM per device.

v0:
```python
import math

import jax
import jax.numpy as jnp
from jax import lax
from jax.sharding import PartitionSpec as P

EPSILON = 1e-06


def copy_for_each(value, axis):
    copies = jnp.broadcast_to(value, (lax.axis_size(axis), *value.shape))
    return lax.all_to_all(copies, axis, split_axis=0, concat_axis=0, tiled=True)


def in_order(blocks, dim):
    lengths = list(blocks.shape[1:])
    lengths[dim] *= blocks.shape[0]
    return jnp.moveaxis(blocks, 0, dim).reshape(lengths)


def gathered_copies(value, axis, dim):
    blocks = copy_for_each(value, axis)
    return in_order(blocks, dim)


def gather_turned(arrays, axis, dims):
    turned = [jnp.moveaxis(a, dim, 0) for a, dim in zip(arrays, dims)]
    widths = [t[0].size for t in turned]
    both = jnp.concatenate([t.reshape(-1, w) for t, w in zip(turned, widths)], axis=1)
    out = lax.all_gather(both, axis, axis=0, tiled=True)
    blocks = jnp.split(out, [sum(widths[:k]) for k in range(1, len(widths))], axis=1)
    return tuple(
        (
            jnp.moveaxis(b.reshape(-1, *t.shape[1:]), 0, dim)
            for b, t, dim in zip(blocks, turned, dims)
        )
    )


def sent_together(arrays, axis, dim, along):
    both = jnp.concatenate(arrays, axis=along)
    out, at, done = (lax.all_gather(both, axis, axis=dim, tiled=True), 0, [])
    for a in arrays:
        done.append(lax.slice_in_dim(out, at, at + a.shape[along], axis=along))
        at += a.shape[along]
    return tuple(done)


def split_up(value, dim, peers):
    lengths = value.shape
    blocks = value.reshape(*lengths[:dim], peers, lengths[dim] // peers, *lengths[dim + 1 :])
    return jnp.moveaxis(blocks, dim, 0)


def summed_on_arrival(value, axis, dim):
    peers = lax.axis_size(axis)
    blocks = lax.all_to_all(split_up(value, dim, peers), axis, 0, 0, tiled=True)
    return jnp.sum(blocks.astype(jnp.float32), axis=0)


def modulate(tokens, shift_mod, scale_mod):
    values = tokens.astype(jnp.float32)
    center = jnp.mean(values, axis=-1, keepdims=True)
    spread = jnp.mean(jnp.square(values - center), axis=-1, keepdims=True)
    normed = (values - center) / jnp.sqrt(spread + EPSILON)
    return (normed * (1.0 + scale_mod[:, None, :]) + shift_mod[:, None, :]).astype(jnp.bfloat16)


def head_norm(projected, gain_vec, head_dim):
    shaped = projected.reshape(projected.shape[:-1] + (projected.shape[-1] // head_dim, head_dim))
    mean_square = jnp.mean(jnp.square(shaped), axis=-1, keepdims=True)
    return (shaped / jnp.sqrt(mean_square + EPSILON) * gain_vec).astype(jnp.bfloat16)


def per_device(
    tokens,
    shift_mod,
    scale_mod,
    gate_mod,
    query_weight,
    key_weight,
    value_weight,
    out_weight,
    query_gain,
    key_gain,
):
    head_dim = query_gain.shape[0]
    modulated = modulate(tokens, shift_mod, scale_mod)
    gathered = gathered_copies(modulated, ("inner", "head"), 1)
    clip_count, row_count, model_width = gathered.shape
    flattened = gathered.reshape(clip_count * row_count, model_width)
    local_cols = query_weight.shape[1]
    head_count = local_cols // head_dim
    full_query, full_key, full_value, full_out = gather_turned(
        (query_weight, key_weight, value_weight, out_weight), "outer", (0, 0, 0, 1)
    )
    query_proj = jnp.dot(flattened, full_query, preferred_element_type=jnp.float32)
    key_proj = jnp.dot(flattened, full_key, preferred_element_type=jnp.float32)
    value_proj = jnp.dot(flattened, full_value, preferred_element_type=jnp.float32)
    query_heads = head_norm(
        query_proj.reshape(clip_count, row_count, local_cols), query_gain, head_dim
    )
    key_send = head_norm(key_proj.reshape(clip_count, row_count, local_cols), key_gain, head_dim)
    key_send = key_send.reshape(clip_count, row_count, local_cols)
    value_send = value_proj.astype(jnp.bfloat16).reshape(clip_count, row_count, local_cols)
    root_size = math.sqrt(head_dim)
    running_max = jnp.full((clip_count, head_count, row_count), -1e30, jnp.float32)
    key_piece, value_piece = sent_together((key_send, value_send), "outer", 1, 0)
    key_count = key_piece.shape[1]
    key_piece = key_piece.reshape(clip_count, key_count, head_count, head_dim)
    value_piece = value_piece.reshape(clip_count, key_count, head_count, head_dim)
    scores = (
        jnp.einsum("cqhd,ckhd->chqk", query_heads, key_piece, preferred_element_type=jnp.float32)
        / root_size
    )
    new_max = jnp.maximum(running_max, jnp.max(scores, axis=-1))
    weights = jnp.exp(scores - new_max[..., None])
    new_sum = jnp.sum(weights, axis=-1)
    new_acc = jnp.einsum(
        "chqk,ckhd->chqd",
        weights.astype(jnp.bfloat16),
        value_piece,
        preferred_element_type=jnp.float32,
    )
    head_out = new_acc / new_sum[..., None]
    mixed = (
        jnp.transpose(head_out, (0, 2, 1, 3))
        .reshape(clip_count * row_count, local_cols)
        .astype(jnp.bfloat16)
    )
    partial_value = jnp.dot(mixed, full_out, preferred_element_type=jnp.float32).reshape(
        clip_count, row_count, -1
    )
    summed = summed_on_arrival(partial_value.astype(jnp.bfloat16), ("inner", "head"), 1)
    return (summed * gate_mod[:, None, :]).astype(jnp.bfloat16)


def solution(mesh):
    in_specs = (
        P("clip", ("outer", "inner", "head"), None),
        P("clip", None),
        P("clip", None),
        P("clip", None),
        P("outer", ("inner", "head")),
        P("outer", ("inner", "head")),
        P("outer", ("inner", "head")),
        P(("inner", "head"), "outer"),
        P(),
        P(),
    )
    out_specs = P("clip", ("outer", "inner", "head"), None)
    return jax.shard_map(
        per_device, mesh=mesh, in_specs=in_specs, out_specs=out_specs, check_vma=False
    )
```

profile of v0, /device:TPU:33, one launch (start us, length us, event | category | flops | bytes accessed | tf_op | source)
XLA Modules:
  0.0 384.0 jit_solution(11839770865233369172)
XLA Ops:
  6.6 1.7 pad_maximum_fusion
  8.4 1.0 convert_reduce_fusion.1
  9.4 1.1 fusion.26
  10.5 0.7 broadcast_add_fusion
  11.2 1.0 fusion.31
  12.2 1.0 broadcast_in_dim.4
  13.2 44.9 %all-to-all-start = ((bf16[8,1,16,3072]{3,2,1,0:T(8,128)(2,1)}), bf16[8,1,16,3072]{3,2,1,0:T(8,128)(2,1)S(1)}, u32[]{:S(2)}, u32[]{:S(2)}) async-start(bf16[8,1,16,3072]{3,2,1,0:T(8,128)(2,1)} %broadcast_in_dim.4), calls=%async_computation | async-start | bytes 1572864 | tf_op jit(solution)/shard_map/all_to_all | solution.py:13
  58.1 12.2 %all-to-all-done = bf16[8,1,16,3072]{3,2,1,0:T(8,128)(2,1)S(1)} async-done(((bf16[8,1,16,3072]{3,2,1,0:T(8,128)(2,1)}), bf16[8,1,16,3072]{3,2,1,0:T(8,128)(2,1)S(1)}, u32[]{:S(2)}, u32[]{:S(2)}) %all-to-all-start) | async-done | bytes 786464 | tf_op jit(solution)/shard_map/all_to_all | solution.py:13
  70.3 99.0 %all-gather.3.cloned.1.call-done = bf16[3072,1536]{1,0:T(8,128)(2,1)} async-done(((bf16[96,1536]{1,0:T(8,128)(2,1)}), bf16[3072,1536]{1,0:T(8,128)(2,1)}) %all-gather.3.cloned.1.call-update) | async-done | bytes 9437200 | tf_op jit(solution)/shard_map/all_gather | solution.py:31
  169.4 2.3 fusion.36
  172.0 2.3 fusion.15
  174.3 0.7 pad_maximum_fusion.1
  175.0 2.3 fusion.37
  177.6 132.8 %all-gather.5.cloned.1.call-done = bf16[2,4096,384]{2,1,0:T(8,128)(2,1)} async-done(((bf16[2,128,384]{2,1,0:T(8,128)(2,1)}), bf16[2,4096,384]{2,1,0:T(8,128)(2,1)}) %all-gather.5.cloned.1.call-update) | async-done | bytes 6291472 | tf_op jit(solution)/shard_map/all_gather | solution.py:43
  310.4 5.1 %fusion.35 = (bf16[1,4096,384]{2,1,0:T(8,128)(2,1)}, bf16[1,4096,384]{2,1,0:T(8,128)(2,1)S(1)}) fusion(bf16[2,4096,384]{2,1,0:T(8,128)(2,1)} %all-gather.5.cloned.1.call-done), kind=kLoop, calls=%fused_computation.44 | loop fusion | bytes 12582912 | tf_op jit(solution)/shard_map/slice | solution.py:45
  315.6 4.7 %copy.27 = bf16[1,4096,384]{1,2,0:T(8,128)(2,1)} copy(bf16[1,4096,384]{2,1,0:T(8,128)(2,1)} %get-tuple-element.5) | data formatting | bytes 6291456 | tf_op jit(solution)/shard_map/slice | solution.py:45
  320.3 5.7 %fusion.38 = (f32[3,128]{1,0:T(4,128)S(1)}, f32[3,128,4096]{2,1,0:T(8,128)}) fusion(bf16[4096,3,128]{0,2,1:T(8,128)(2,1)} %bitcast.37, f32[128,3,128]{0,2,1:T(8,128)S(1)} %bitcast.46, f32[128]{0:T(128)S(1)} %copy-done.3, f32[128,3]{0,1:T(4,128)S(1)} %add_sqrt_fusion.1), kind=kOutput, calls=%fused_computation.47 | convolution fusion | flops 405945984 | bytes 9637376 | tf_op jit(solution)/shard_map/cqhd,ckhd->chqk/dot_general | solution.py:114
  326.0 2.9 copy.30
  328.9 3.9 %fusion = f32[3,128]{1,0:T(4,128)S(1)} fusion(f32[3,128,4096]{2,1,0:T(8,128)} %get-tuple-element.12, f32[3,128]{1,0:T(4,128)S(1)} %broadcast_maximum_fusion), kind=kLoop, calls=%fused_computation.2 | loop fusion | flops 3145344 | bytes 6294528 | tf_op jit(solution)/shard_map/reduce_sum | solution.py:119
  332.8 0.7 copy-done.1
  333.5 3.2 fusion.21
  336.7 2.5 convolution_convert_fusion
  339.3 37.1 %all_to_all.10 = bf16[8,1,16,3072]{3,2,1,0:T(8,128)(2,1)S(1)} all-to-all(bf16[8,1,16,3072]{3,2,1,0:T(8,128)(2,1)S(1)} %bitcast.39), channel_id=1, replica_groups=mesh['clip'=2,'outer'=32,'inner'=4,'head'=2] {'inner','head'}, dimensions={0} | all-to-all | bytes 1572864 | tf_op jit(solution)/shard_map/all_to_all | solution.py:58
  376.5 0.7 fusion.30
  (26 shorter events, 0.9 us)
Async XLA Ops:
  6.5 51.5 %copy-start = (f32[128]{0:T(128)S(1)}, f32[128]{0:T(128)}, u32[]{:S(2)}) copy-start(f32[128]{0:T(128)} %param.19) | copy-start | bytes 1540
  6.6 162.8 %all-gather.3.cloned.1.call-start = ((), (), s32[]{:S(2)}) async-start(), calls=%async_computation.2 | async-start | bytes 9732096 | tf_op jit(solution)/shard_map/all_gather | solution.py:31
  13.2 57.1 %all-to-all-start = ((bf16[8,1,16,3072]{3,2,1,0:T(8,128)(2,1)}), bf16[8,1,16,3072]{3,2,1,0:T(8,128)(2,1)S(1)}, u32[]{:S(2)}, u32[]{:S(2)}) async-start(bf16[8,1,16,3072]{3,2,1,0:T(8,128)(2,1)} %broadcast_in_dim.4), calls=%async_computation | async-start | bytes 1572864 | tf_op jit(solution)/shard_map/all_to_all | solution.py:13
  58.1 252.3 %all-gather.5.cloned.1.call-start = ((), (), s32[]{:S(2)}) async-start(), calls=%async_computation.3 | async-start | bytes 6488064 | tf_op jit(solution)/shard_map/all_gather | solution.py:43
  315.6 4.7 %copy-start.3 = (f32[128]{0:T(128)S(1)}, f32[128]{0:T(128)}, u32[]{:S(2)}) copy-start(f32[128]{0:T(128)} %param.18) | copy-start | bytes 1540
  328.9 4.6 %copy-start.1 = (f32[3,128,4096]{2,1,0:T(8,128)S(1)}, f32[3,128,4096]{2,1,0:T(8,128)}, u32[]{:S(2)}) copy-start(f32[3,128,4096]{2,1,0:T(8,128)} %get-tuple-element.12) | copy-start | bytes 18874372
  333.5 43.0 %copy-start.2 = (f32[1,3072]{1,0:T(1,128)S(1)}, f32[1,3072]{1,0:T(1,128)}, u32[]{:S(2)}) copy-start(f32[1,3072]{1,0:T(1,128)} %param.13) | copy-start | bytes 36868
Sparse Core Ops, SparseCore 0:
  9.4 159.8 all-gather.2
  175.2 135.2 all-gather.4
where the time goes:
time: 385 us; the launch traced here: 384 us
  waiting for transfers between devices  244 us (63%)
  starting transfers between devices  44.9 us (12%)
  blocking collectives  37.1 us (10%)
  matrix products  18.3 us (5%)
  local copies, waits for them, and re-layouts  14.9 us (4%)
  between operations  13.5 us (4%)
  other arithmetic  11.1 us (3%)
    all_gather x1, waiting for transfers between devices, sent_together(): out, at, done = (lax.all_gather(both, axis, axis=dim, tiled=True), 0, [])  133 us
    all_gather x1, waiting for transfers between devices, gather_turned(): out = lax.all_gather(both, axis, axis=0, tiled=True)  99 us
    all_to_all x1, starting transfers between devices, copy_for_each(): return lax.all_to_all(copies, axis, split_axis=0, concat_axis=0, tiled=True)  44.9 us
    all_to_all x1, blocking collectives, summed_on_arrival(): blocks = lax.all_to_all(split_up(value, dim, peers), axis, 0, 0, tiled=True)  37.1 us
    slice x3, local copies, waits for them, and re-layouts, sent_together(): done.append(lax.slice_in_dim(out, at, at + a.shape[along], axis=along))  12.7 us
    all_to_all x1, waiting for transfers between devices, copy_for_each(): return lax.all_to_all(copies, axis, split_axis=0, concat_axis=0, tiled=True)  12.2 us
  transfers between devices with their start and end apart: 3, of which 3 were waited for; matrix products, arithmetic and copies ran while one was open for 2% of the time, Pallas kernels for 0%

commit v1 on v0

v1 whole, which is shorter than its diff:
```python
import math

import jax
import jax.numpy as jnp
from jax import lax
from jax.experimental import pallas as pl
from jax.experimental.pallas import tpu as pltpu
from jax.sharding import Mesh
from jax.sharding import PartitionSpec as P

EPSILON = 1e-06
BIG = 8
OUTER = ("big", "zh", "zn")
INNER = ("xt", "xu")
GROUP = (*OUTER, *INNER, "head")
FAR = ("big", "zh")
EIGHT = ("zn", *INNER)


def at(place, sizes):
    index = 0
    for p, s in zip(place, sizes):
        index = index * s + p
    return index


def places(sizes):
    if not sizes:
        yield ()
        return
    for first in range(sizes[0]):
        for rest in places(sizes[1:]):
            yield (first, *rest)


def swapped(value, axes):
    n = lax.axis_size(axes)
    return lax.ppermute(value, axes, [(i, n - 1 - i) for i in range(n)])


def around(value, axes, shift):
    n = lax.axis_size(axes)
    return lax.ppermute(value, axes, [(i, (i + shift) % n) for i in range(n)])


def modulate_body(tok_ref, scale_ref, shift_ref, rider_ref, out_ref):
    values = tok_ref[...].astype(jnp.float32)
    width = values.shape[1]
    center = jnp.mean(values, axis=-1, keepdims=True)
    spread = jnp.mean(jnp.square(values - center), axis=-1, keepdims=True)
    normed = (values - center) / jnp.sqrt(spread + EPSILON)
    out_ref[:, :width] = (normed * (1.0 + scale_ref[...]) + shift_ref[...]).astype(jnp.bfloat16)
    out_ref[:, width:] = rider_ref[...]


def modulate(tokens, scale_mod, shift_mod, rider):
    return pl.pallas_call(
        modulate_body,
        out_shape=jax.ShapeDtypeStruct(
            (tokens.shape[0], tokens.shape[1] + rider.shape[1]), jnp.bfloat16
        ),
        name="modulate",
    )(tokens, scale_mod, shift_mod, rider)


def project_body(order_ref, *refs, parts, pieces, head_dim):
    toks, w_refs = refs[:parts], refs[parts : parts + pieces]
    qg_ref, kg_ref, q_ref, kv_ref = refs[parts + pieces :]
    depth = w_refs[0].shape[-2]

    def norm(shaped, gain):
        mean_square = jnp.mean(jnp.square(shaped), axis=-1, keepdims=True)
        return (shaped / jnp.sqrt(mean_square + EPSILON) * gain).astype(jnp.bfloat16)

    row = 0
    for tok in toks:
        acc, k = None, 0
        for w_ref in w_refs:
            for s in range(w_ref.shape[0]):
                start = pl.multiple_of(order_ref[k] * depth, 128)
                term = jnp.dot(
                    tok[:, pl.ds(start, depth)], w_ref[s], preferred_element_type=jnp.float32
                )
                acc, k = term if acc is None else acc + term, k + 1
        mine = slice(row, row + tok.shape[0])
        q_ref[mine, :] = norm(acc[:, :head_dim], qg_ref[...])
        kv_ref[mine, :head_dim] = norm(acc[:, head_dim : 2 * head_dim], kg_ref[...])
        kv_ref[mine, head_dim:] = acc[:, 2 * head_dim :].astype(jnp.bfloat16)
        row += tok.shape[0]


def project(order, toks, weights, query_gain, key_gain, head_dim):
    rows = sum(t.shape[0] for t in toks)
    vmem = pl.BlockSpec(memory_space=pltpu.VMEM)
    smem = pl.BlockSpec(memory_space=pltpu.SMEM)
    return pl.pallas_call(
        lambda *refs: project_body(
            *refs, parts=len(toks), pieces=len(weights), head_dim=head_dim
        ),
        in_specs=[smem] + [vmem] * (len(toks) + len(weights) + 2),
        out_shape=(
            jax.ShapeDtypeStruct((rows, head_dim), jnp.bfloat16),
            jax.ShapeDtypeStruct((rows, 2 * head_dim), jnp.bfloat16),
        ),
        name="project",
    )(order, *toks, *weights, query_gain[None], key_gain[None])


def attend_body(q_ref, *refs, head_dim, chunk):
    *kv_refs, out_ref, score_ref = refs
    root = math.sqrt(head_dim)
    q = q_ref[...]
    top, at_key, spots = None, 0, []
    for kv in kv_refs:
        step = min(chunk, kv.shape[0])
        for start in range(0, kv.shape[0], step):
            keys = kv[start : start + step, :head_dim]
            s = (
                lax.dot_general(
                    q, keys, (((1,), (1,)), ((), ())), preferred_element_type=jnp.float32
                )
                / root
            )
            score_ref[:, at_key : at_key + step] = s
            m = jnp.max(s, axis=-1, keepdims=True)
            top = m if top is None else jnp.maximum(top, m)
            spots.append((kv, start, at_key, step))
            at_key += step
    total, acc = None, None
    for kv, start, spot, step in spots:
        w = jnp.exp(score_ref[:, spot : spot + step] - top)
        part = jnp.sum(w, axis=-1, keepdims=True)
        term = jnp.dot(
            w.astype(jnp.bfloat16),
            kv[start : start + step, head_dim:],
            preferred_element_type=jnp.float32,
        )
        total = part if total is None else total + part
        acc = term if acc is None else acc + term
    out_ref[...] = (acc / total).astype(jnp.bfloat16)


def attend(query, kvs, head_dim):
    rows = 128
    keys = sum(kv.shape[0] for kv in kvs)
    whole = [pl.BlockSpec(kv.shape, lambda i: (0, 0)) for kv in kvs]
    return pl.pallas_call(
        lambda *refs: attend_body(*refs, head_dim=head_dim, chunk=512),
        grid=(query.shape[0] // rows,),
        in_specs=[pl.BlockSpec((rows, head_dim), lambda i: (i, 0))] + whole,
        out_specs=pl.BlockSpec((rows, head_dim), lambda i: (i, 0)),
        scratch_shapes=[pltpu.VMEM((rows, keys), jnp.float32)],
        out_shape=jax.ShapeDtypeStruct(query.shape, jnp.bfloat16),
        name="attend",
    )(query, *kvs)


def combine_body(order_ref, mixed_ref, *refs):
    *w_refs, gate_ref, out_ref = refs
    summed, k = None, 0
    for w_ref in w_refs:
        depth = w_ref.shape[-1]
        for s in range(w_ref.shape[0]):
            start = pl.multiple_of(order_ref[k] * depth, 128)
            term = lax.dot_general(
                mixed_ref[:, pl.ds(start, depth)],
                w_ref[s],
                (((1,), (1,)), ((), ())),
                preferred_element_type=jnp.float32,
            )
            term = term.astype(jnp.bfloat16).astype(jnp.float32)
            summed, k = term if summed is None else summed + term, k + 1
    out_ref[...] = (summed * gate_ref[...]).astype(jnp.bfloat16)


def combine(order, mixed, weights, gate):
    vmem = pl.BlockSpec(memory_space=pltpu.VMEM)
    smem = pl.BlockSpec(memory_space=pltpu.SMEM)
    return pl.pallas_call(
        combine_body,
        in_specs=[smem] + [vmem] * (len(weights) + 2),
        out_shape=jax.ShapeDtypeStruct((mixed.shape[0], gate.shape[1]), jnp.bfloat16),
        name="combine",
    )(order, mixed, *weights, gate)


def weights_to_tile(packed, sizes):
    turn, move = [], []
    for b, zh, zn, xt, xu, c in places(sizes):
        here = at((b, zh, zn, xt, xu, c), sizes)
        pt, pu = xt ^ (b % 2), xu ^ zn
        there = at((b, zh, zn, pt, pu, c), sizes)
        group = at((xt, xu, c), sizes[3:])
        turn.append((here, there))
        move.append((there, at((group, zh, b // 2 % 2, pt, pu, b // 4), sizes)))
    moved = lax.ppermute(packed, GROUP, turn)
    moved = lax.ppermute(moved, GROUP, move)
    tiles = sizes[1] * sizes[4]
    spare = tiles - moved.shape[0]
    moved = jnp.concatenate([moved, jnp.zeros((spare, *moved.shape[1:]), moved.dtype)], axis=0)
    mine = lax.all_to_all(moved, ("zh", "xu"), 0, 0, tiled=True)
    mine = mine.reshape(sizes[1], sizes[4], *packed.shape[1:])
    odd = lax.axis_index("big") // sizes[5] % 2 == 1
    return jnp.where(odd, mine[:, ::-1], mine).reshape(1, -1, packed.shape[-1])


def per_device(
    tokens,
    shift_mod,
    scale_mod,
    gate_mod,
    query_weight,
    key_weight,
    value_weight,
    out_weight,
    query_gain,
    key_gain,
):
    head_dim = query_gain.shape[0]
    sizes = tuple(lax.axis_size(a) for a in GROUP)
    far, inner, head = lax.axis_size(FAR), lax.axis_size(INNER), sizes[5]
    clips, own, width = tokens.shape
    local_cols = query_weight.shape[1]
    head_count = local_cols // head_dim
    big, zn, xt, xu, zc = (lax.axis_index(a) for a in ("big", "zn", "xt", "xu", "head"))
    zx = lax.axis_index(INNER)

    rider = out_weight.T.reshape(own, -1)
    modulated = modulate(tokens.reshape(own, width), scale_mod, shift_mod, rider)
    gathered = lax.all_gather(modulated, FAR, axis=0, tiled=True)
    mine = gathered[:, :width]
    half = mine.shape[0] // 2
    left = around(mine[:half], INNER, 1)
    right = around(mine[half:], INNER, -1)

    packed = jnp.stack(
        [
            jnp.concatenate(
                [w[:, i * head_dim : (i + 1) * head_dim] for w in (query_weight, key_weight, value_weight)],
                axis=1,
            )
            for i in range(head_count)
        ]
    )
    piece = weights_to_tile(packed, sizes)
    near = [piece, swapped(piece, "zn"), swapped(piece, "xt"), None]
    near[3] = lax.ppermute(piece, ("zn", "xt"), [(i, 3 - i) for i in range(4)])
    stack = jnp.concatenate(near, axis=0)
    weights = [stack, swapped(stack, "head")]
    odd_t = big // (2 * head)
    spot = [(xt ^ t ^ odd_t) + 2 * (zn ^ n) for n, t in ((0, 0), (1, 0), (0, 1), (1, 1))]
    order = jnp.stack([s + 4 * c for c in (zc, 1 - zc) for s in spot]).astype(jnp.int32)

    def exchanged(kv):
        near = [kv, swapped(kv, "zn"), swapped(kv, "xt")]
        near.append(lax.ppermute(kv, ("zn", "xt"), [(i, 3 - i) for i in range(4)]))
        return [*near, swapped(jnp.concatenate(near), "head")]

    query_a, kv_a = project(order, [mine], weights, query_gain, key_gain, head_dim)
    kvs = exchanged(kv_a)
    query_b, kv_b = project(order, [left, right], weights, query_gain, key_gain, head_dim)
    kvs = kvs + exchanged(kv_b)
    heads_out = attend(jnp.concatenate([query_a, query_b]), kvs, head_dim)

    ours, to_left, to_right = heads_out[: 2 * half], heads_out[2 * half : 3 * half], heads_out[3 * half :]
    theirs = jnp.concatenate([around(to_left, INNER, -1), around(to_right, INNER, 1)])
    pair = jnp.where(
        xu == 0, jnp.concatenate([ours, theirs], axis=1), jnp.concatenate([theirs, ours], axis=1)
    )
    back = lax.all_to_all(pair.reshape(far, own, 2 * head_dim), FAR, 0, 0, tiled=True)
    back = back.reshape(sizes[0], sizes[1], own, 2, head_dim)
    back = jnp.transpose(back, (2, 0, 1, 3, 4)).reshape(own, sizes[0], -1)[:, :, :local_cols]
    mixed = lax.all_gather(back.reshape(own, width), EIGHT, axis=0, tiled=True)

    out_far, _ = lax.optimization_barrier((gathered[:, width:], heads_out))
    out_far = out_far.reshape(-1, out_weight.shape[0])
    block = out_far.shape[0] // inner
    got = []
    for s in range(inner):
        send = lax.dynamic_slice_in_dim(out_far, (zx + s) % inner * block, block, axis=0)
        got.append((around(send, INNER, s) if s else send)[None])
    outs = jnp.concatenate(got, axis=0)
    outs = [outs, swapped(outs, "head")]
    source = [(zx - s) % inner * head for s in range(inner)]
    out_order = jnp.stack([s + c for c in (zc, 1 - zc) for s in source]).astype(jnp.int32)
    gate = gate_mod.reshape(inner, far // inner, sizes[2], -1)
    gate = lax.dynamic_index_in_dim(gate, zx, 0, keepdims=False)
    gate = lax.dynamic_index_in_dim(gate, zn, 1, keepdims=False).reshape(1, block)
    done = combine(out_order, mixed, outs, gate)
    done = lax.all_to_all(done.reshape(-1, own, block), EIGHT, 0, 0, tiled=True)
    done = done.reshape(sizes[2], inner, own, far // inner, -1)
    return jnp.transpose(done, (2, 1, 3, 0, 4)).reshape(clips, own, width)


def solution(mesh):
    shape = mesh.shape
    inner = shape["inner"]
    split = (shape["clip"], BIG, 2, shape["outer"] // (2 * BIG), 2, inner // 2, shape["head"])
    fine = Mesh(mesh.devices.reshape(split), ("clip", *GROUP))
    row = (*INNER, "head")
    in_specs = (
        P("clip", GROUP, None),
        P("clip", None),
        P("clip", None),
        P("clip", None),
        P(OUTER, row),
        P(OUTER, row),
        P(OUTER, row),
        P(row, OUTER),
        P(),
        P(),
    )

    return jax.shard_map(
        per_device,
        mesh=fine,
        in_specs=in_specs,
        out_specs=P("clip", GROUP, None),
        check_vma=False,
    )
```

time: 385 us -> 350 us (0.909)
  the two profiles are of different devices: /device:TPU:33 before, /device:TPU:34 now
where the time goes in v1:
time: 350 us; the launch traced here: 348 us
  starting transfers between devices  148 us (42%)
  waiting for transfers between devices  97.1 us (28%)
  blocking collectives  43.9 us (13%)
  local copies, waits for them, and re-layouts  21 us (6%)
  Pallas kernels  20.6 us (6%)
  between operations  14.2 us (4%)
    ppermute x10, starting transfers between devices, swapped(): return lax.ppermute(value, axes, [(i, n - 1 - i) for i in range(n)])  45.9 us
    all_gather x1, blocking collectives, per_device(): mixed = lax.all_gather(back.reshape(own, width), EIGHT, axis=0, tiled=True)  31.3 us
    ppermute x1, starting transfers between devices, per_device(): near[3] = lax.ppermute(piece, ('zn', 'xt'), [(i, 3 - i) for i in range(4)])  23.7 us
    ppermute x1, starting transfers between devices, weights_to_tile(): moved = lax.ppermute(moved, GROUP, move)  22.6 us
    ppermute x7, starting transfers between devices, around(): return lax.ppermute(value, axes, [(i, (i + shift) % n) for i in range(n)])  22 us
    all_to_all x1, waiting for transfers between devices, per_device(): lax.all_to_all(pair.reshape(far, own, 2 * head_dim), FAR, 0, 0, tiled=True)  21.6 us
    all_to_all x1, waiting for transfers between devices, weights_to_tile(): mine = lax.all_to_all(moved, ('zh', 'xu'), 0, 0, tiled=True)  18.8 us
    all_to_all x1, starting transfers between devices, weights_to_tile(): mine = lax.all_to_all(moved, ('zh', 'xu'), 0, 0, tiled=True)  18.4 us
  transfers between devices with their start and end apart: 25, of which 9 were waited for; matrix products, arithmetic and copies ran while one was open for 4% of the time, Pallas kernels for 2%

profile of v1, /device:TPU:34, one launch (start us, length us, event | category | flops | bytes accessed | tf_op | source)
XLA Modules:
  0.0 348.5 jit_solution(9921322944901460721)
XLA Ops:
  13.2 22.6 %collective-permute-start.1 = (bf16[3,96,384]{2,1,0:T(8,128)(2,1)S(1)}, bf16[3,96,384]{2,1,0:T(8,128)(2,1)S(1)}, u32[]{:S(2)}, u32[]{:S(2)}) collective-permute-start(bf16[3,96,384]{2,1,0:T(8,128)(2,1)S(1)} %collective-permute-done), channel_id=1, source_target_pairs={{0,0},{1,32},{2,66},{3,98},{4,132},{5,164},{6,198},{7,230},{10,2},... | collective-permute-start | bytes 663560 | tf_op jit(solution)/shard_map/ppermute | solution.py:197
  35.9 3.5 collective-permute-done.1
  40.1 18.4 %all-to-all-start = ((bf16[4,96,384]{2,1,0:T(8,128)(2,1)}), bf16[4,96,384]{2,1,0:T(8,128)(2,1)S(1)}, u32[]{:S(2)}, u32[]{:S(2)}) async-start(bf16[4,96,384]{2,1,0:T(8,128)(2,1)} %concatenate.45), calls=%async_computation | async-start | bytes 589824 | tf_op jit(solution)/shard_map/all_to_all | solution.py:201
  58.5 18.8 %all-to-all-done = bf16[4,96,384]{2,1,0:T(8,128)(2,1)S(1)} async-done(((bf16[4,96,384]{2,1,0:T(8,128)(2,1)}), bf16[4,96,384]{2,1,0:T(8,128)(2,1)S(1)}, u32[]{:S(2)}, u32[]{:S(2)}) %all-to-all-start) | async-done | bytes 294944 | tf_op jit(solution)/shard_map/all_to_all | solution.py:201
  77.4 23.7 %collective-permute-start.4 = (bf16[1,384,384]{2,1,0:T(8,128)(2,1)S(1)}, bf16[1,384,384]{2,1,0:T(8,128)(2,1)S(1)}, u32[]{:S(2)}, u32[]{:S(2)}) collective-permute-start(bf16[1,384,384]{2,1,0:T(8,128)(2,1)S(1)} %bitcast.47), channel_id=1, source_target_pairs={{0,12},{4,8},{8,4},{12,0},{1,13},{5,9},{9,5},{13,1},{2,14},{6,10},... | collective-permute-start | bytes 884744 | tf_op jit(solution)/shard_map/ppermute | solution.py:247
  103.5 3.4 collective-permute-start.2
  106.9 7.2 %collective-permute-done.4 = bf16[1,384,384]{2,1,0:T(8,128)(2,1)S(1)} collective-permute-done((bf16[1,384,384]{2,1,0:T(8,128)(2,1)S(1)}, bf16[1,384,384]{2,1,0:T(8,128)(2,1)S(1)}, u32[]{:S(2)}, u32[]{:S(2)}) %collective-permute-start.4) | collective-permute-done | bytes 294944 | tf_op jit(solution)/shard_map/ppermute | solution.py:247
  114.0 15.5 %collective-permute-done.2 = bf16[1,384,384]{2,1,0:T(8,128)(2,1)S(1)} collective-permute-done((bf16[1,384,384]{2,1,0:T(8,128)(2,1)S(1)}, bf16[1,384,384]{2,1,0:T(8,128)(2,1)S(1)}, u32[]{:S(2)}, u32[]{:S(2)}) %collective-permute-start.2) | collective-permute-done | bytes 294944 | tf_op jit(solution)/shard_map/ppermute | solution.py:38
  129.7 15.6 %collective-permute-start.5 = (bf16[4,384,384]{2,1,0:T(8,128)(2,1)S(1)}, bf16[4,384,384]{2,1,0:T(8,128)(2,1)S(1)}, u32[]{:S(2)}, u32[]{:S(2)}) collective-permute-start(bf16[4,384,384]{2,1,0:T(8,128)(2,1)S(1)} %pad_maximum_fusion.refs_2_.refs_3_), channel_id=1, source_target_pairs={{0,1},{1,0},{2,3},{3,2},{4,5},{5,4},{6,7},{7,6},{8,9},{9,8},{10,11... | collective-permute-start | bytes 3538952 | tf_op jit(solution)/shard_map/ppermute | solution.py:38
  145.3 17.2 %all-gather.2.cloned.1.call-done = bf16[256,5376]{1,0:T(8,128)(2,1)} async-done(((bf16[16,5376]{1,0:T(8,128)(2,1)}), bf16[256,5376]{1,0:T(8,128)(2,1)}) %all-gather.2.cloned.1.call-update) | async-done | bytes 2752528 | tf_op jit(solution)/shard_map/all_gather | solution.py:230
  165.2 5.6 %collective-permute-start.6 = (bf16[128,3072]{1,0:T(8,128)(2,1)}, bf16[128,3072]{1,0:T(8,128)(2,1)S(1)}, u32[]{:S(2)}, u32[]{:S(2)}) collective-permute-start(bf16[128,3072]{1,0:T(8,128)(2,1)} %get-tuple-element.16), channel_id=1, source_target_pairs={{0,2},{2,4},{4,6},{6,0},{1,3},{3,5},{5,7},{7,1},{8,10},{10,12},{12... | collective-permute-start | bytes 2359304 | tf_op jit(solution)/shard_map/ppermute | solution.py:43
  177.2 4.0 %project.2 = (bf16[256,128]{1,0:T(8,128)(2,1)}, bf16[256,256]{1,0:T(8,128)(2,1)}) custom-call(s32[8]{0:T(128)} %stack.83.refs_0_, bf16[256,3072]{1,0:T(8,128)(2,1)} %slice.70.refs_1_, bf16[4,384,384]{2,1,0:T(8,128)(2,1)} %copy-done, bf16[4,384,384]{2,1,0:T(8,128)(2,1)} %copy-done.1, f32[1,128]{1,0:T(1,128)} %bitcast.65, f32[1,128]{1,0:T(1,128)} %bitcast.67), custom_call_target="tpu_custom_call" | custom-call | tf_op jit(solution)/shard_map/project/pallas_call | solution.py:96
  183.3 7.7 %collective-permute-start.9 = (bf16[256,256]{1,0:T(8,128)(2,1)}, bf16[256,256]{1,0:T(8,128)(2,1)S(1)}, u32[]{:S(2)}, u32[]{:S(2)}) collective-permute-start(bf16[256,256]{1,0:T(8,128)(2,1)} %get-tuple-element.12.refs_1_), channel_id=1, source_target_pairs={{0,4},{4,0},{1,5},{5,1},{2,6},{6,2},{3,7},{7,3},{8,12},{12,8},{9,1... | collective-permute-start | bytes 393224 | tf_op jit(solution)/shard_map/ppermute | solution.py:38
  193.9 4.1 %project.3 = (bf16[256,128]{1,0:T(8,128)(2,1)}, bf16[256,256]{1,0:T(8,128)(2,1)}) custom-call(s32[8]{0:T(128)} %stack.83.refs_0_, bf16[128,3072]{1,0:T(8,128)(2,1)} %copy-done.4, bf16[128,3072]{1,0:T(8,128)(2,1)} %collective-permute-done.7.refs_2_, bf16[4,384,384]{2,1,0:T(8,128)(2,1)} %copy-done, bf16[4,384,384]{2,1,0:T(8,128)(2,1)} %copy-done.1, ...), custom_call_target="tpu_custom_call" | custom-call | tf_op jit(solution)/shard_map/project/pallas_call | solution.py:96
  201.3 5.5 %collective-permute-start.13 = (bf16[256,256]{1,0:T(8,128)(2,1)}, bf16[256,256]{1,0:T(8,128)(2,1)S(1)}, u32[]{:S(2)}, u32[]{:S(2)}) collective-permute-start(bf16[256,256]{1,0:T(8,128)(2,1)} %get-tuple-element.13.refs_6_), channel_id=1, source_target_pairs={{0,4},{4,0},{1,5},{5,1},{2,6},{6,2},{3,7},{7,3},{8,12},{12,8},{9,1... | collective-permute-start | bytes 393224 | tf_op jit(solution)/shard_map/ppermute | solution.py:38
  210.9 5.4 %collective-permute-done.14.refs_9_ = bf16[256,256]{1,0:T(8,128)(2,1)S(1)} collective-permute-done((bf16[256,256]{1,0:T(8,128)(2,1)}, bf16[256,256]{1,0:T(8,128)(2,1)S(1)}, u32[]{:S(2)}, u32[]{:S(2)}) %collective-permute-start.14) | collective-permute-done | bytes 131104 | tf_op jit(solution)/shard_map/ppermute | solution.py:256
  223.1 7.2 %attend.1 = bf16[512,128]{1,0:T(8,128)(2,1)} custom-call(bf16[512,128]{1,0:T(8,128)(2,1)} %pad_maximum_fusion.5.refs_0_, bf16[256,256]{1,0:T(8,128)(2,1)} %get-tuple-element.12.refs_1_, bf16[256,256]{1,0:T(8,128)(2,1)} %copy-done.9, bf16[256,256]{1,0:T(8,128)(2,1)} %copy-done.10, bf16[256,256]{1,0:T(8,128)(2,1)} %copy-done.11, bf16[1024,256]{1,0:T(8,128)(2,1)} %copy-done.6, ...), custom_call_target="tpu_custom_call" | custom-call | tf_op jit(solution)/shard_map/attend/pallas_call | solution.py:147
  234.1 3.4 collective-permute-start.19
  240.0 4.0 %collective-permute-start.17 = (bf16[128,128]{1,0:T(8,128)(2,1)S(1)}, bf16[128,128]{1,0:T(8,128)(2,1)S(1)}, u32[]{:S(2)}, u32[]{:S(2)}) collective-permute-start(bf16[128,128]{1,0:T(8,128)(2,1)S(1)} %get-tuple-element.22), channel_id=1, source_target_pairs={{0,2},{2,4},{4,6},{6,0},{1,3},{3,5},{5,7},{7,1},{8,10},{10,12},{12... | collective-permute-start | bytes 98312 | tf_op jit(solution)/shard_map/ppermute | solution.py:43
  246.0 7.6 %collective-permute-done.17 = bf16[128,128]{1,0:T(8,128)(2,1)S(1)} collective-permute-done((bf16[128,128]{1,0:T(8,128)(2,1)S(1)}, bf16[128,128]{1,0:T(8,128)(2,1)S(1)}, u32[]{:S(2)}, u32[]{:S(2)}) %collective-permute-start.17) | collective-permute-done | bytes 32800 | tf_op jit(solution)/shard_map/ppermute | solution.py:43
  254.4 11.1 %all-to-all-start.1 = ((bf16[16,16,256]{2,1,0:T(8,128)(2,1)}), bf16[16,16,256]{2,1,0:T(8,128)(2,1)S(1)}, u32[]{:S(2)}, u32[]{:S(2)}) async-start(bf16[16,16,256]{2,1,0:T(8,128)(2,1)} %maximum_select_fusion), calls=%async_computation.1 | async-start | bytes 262144 | tf_op jit(solution)/shard_map/all_to_all | solution.py:270
  270.4 21.6 %all-to-all-done.1 = bf16[16,16,256]{2,1,0:T(8,128)(2,1)S(1)} async-done(((bf16[16,16,256]{2,1,0:T(8,128)(2,1)}), bf16[16,16,256]{2,1,0:T(8,128)(2,1)S(1)}, u32[]{:S(2)}, u32[]{:S(2)}) %all-to-all-start.1) | async-done | bytes 131104 | tf_op jit(solution)/shard_map/all_to_all | solution.py:270
  292.2 31.3 %all_gather.7.mixed_ref = bf16[128,3072]{1,0:T(8,128)(2,1)} all-gather(bf16[16,3072]{1,0:T(8,128)(2,1)S(1)} %bitcast.57), channel_id=1, replica_groups=mesh['clip'=2,'big'=8,'zh'=2,'zn'=2,'xt'=2,'xu'=2,'head'=2] {'zn','xt','..., dimensions={0}, use_global_device_ids=true | all-gather | bytes 884736 | tf_op jit(solution)/shard_map/all_gather | solution.py:273
  327.8 12.7 %all_to_all.15 = bf16[8,16,384]{2,1,0:T(8,128)(2,1)S(1)} all-to-all(bf16[8,16,384]{2,1,0:T(8,128)(2,1)} %bitcast.55), channel_id=1, replica_groups=mesh['clip'=2,'big'=8,'zh'=2,'zn'=2,'xt'=2,'xu'=2,'head'=2] {'zn','xt','..., dimensions={0} | all-to-all | bytes 196608 | tf_op jit(solution)/shard_map/all_to_all | solution.py:290
  (109 shorter events, 57.4 us)
Async XLA Ops:
  6.5 156.0 %all-gather.2.cloned.1.call-start = ((), (), s32[]{:S(2)}) async-start(), calls=%async_computation.3 | async-start | bytes 2924544 | tf_op jit(solution)/shard_map/all_gather | solution.py:230
  13.2 26.1 %collective-permute-start.1 = (bf16[3,96,384]{2,1,0:T(8,128)(2,1)S(1)}, bf16[3,96,384]{2,1,0:T(8,128)(2,1)S(1)}, u32[]{:S(2)}, u32[]{:S(2)}) collective-permute-start(bf16[3,96,384]{2,1,0:T(8,128)(2,1)S(1)} %collective-permute-done), channel_id=1, source_target_pairs={{0,0},{1,32},{2,66},{3,98},{4,132},{5,164},{6,198},{7,230},{10,2},... | collective-permute-start | bytes 663560 | tf_op jit(solution)/shard_map/ppermute | solution.py:197
  40.1 37.2 %all-to-all-start = ((bf16[4,96,384]{2,1,0:T(8,128)(2,1)}), bf16[4,96,384]{2,1,0:T(8,128)(2,1)S(1)}, u32[]{:S(2)}, u32[]{:S(2)}) async-start(bf16[4,96,384]{2,1,0:T(8,128)(2,1)} %concatenate.45), calls=%async_computation | async-start | bytes 589824 | tf_op jit(solution)/shard_map/all_to_all | solution.py:201
  77.4 36.7 %collective-permute-start.4 = (bf16[1,384,384]{2,1,0:T(8,128)(2,1)S(1)}, bf16[1,384,384]{2,1,0:T(8,128)(2,1)S(1)}, u32[]{:S(2)}, u32[]{:S(2)}) collective-permute-start(bf16[1,384,384]{2,1,0:T(8,128)(2,1)S(1)} %bitcast.47), channel_id=1, source_target_pairs={{0,12},{4,8},{8,4},{12,0},{1,13},{5,9},{9,5},{13,1},{2,14},{6,10},... | collective-permute-start | bytes 884744 | tf_op jit(solution)/shard_map/ppermute | solution.py:247
  101.0 13.0 %collective-permute-start.3 = (bf16[1,384,384]{2,1,0:T(8,128)(2,1)S(1)}, bf16[1,384,384]{2,1,0:T(8,128)(2,1)S(1)}, u32[]{:S(2)}, u32[]{:S(2)}) collective-permute-start(bf16[1,384,384]{2,1,0:T(8,128)(2,1)S(1)} %bitcast.48), channel_id=1, source_target_pairs={{0,4},{4,0},{1,5},{5,1},{2,6},{6,2},{3,7},{7,3},{8,12},{12,8},{9,1... | collective-permute-start | bytes 884744 | tf_op jit(solution)/shard_map/ppermute | solution.py:38
  103.5 26.0 %collective-permute-start.2 = (bf16[1,384,384]{2,1,0:T(8,128)(2,1)S(1)}, bf16[1,384,384]{2,1,0:T(8,128)(2,1)S(1)}, u32[]{:S(2)}, u32[]{:S(2)}) collective-permute-start(bf16[1,384,384]{2,1,0:T(8,128)(2,1)S(1)} %bitcast.49), channel_id=1, source_target_pairs={{0,8},{8,0},{1,9},{9,1},{2,10},{10,2},{3,11},{11,3},{4,12},{12,4},... | collective-permute-start | bytes 884744 | tf_op jit(solution)/shard_map/ppermute | solution.py:38
  129.7 46.5 %collective-permute-start.5 = (bf16[4,384,384]{2,1,0:T(8,128)(2,1)S(1)}, bf16[4,384,384]{2,1,0:T(8,128)(2,1)S(1)}, u32[]{:S(2)}, u32[]{:S(2)}) collective-permute-start(bf16[4,384,384]{2,1,0:T(8,128)(2,1)S(1)} %pad_maximum_fusion.refs_2_.refs_3_), channel_id=1, source_target_pairs={{0,1},{1,0},{2,3},{3,2},{4,5},{5,4},{6,7},{7,6},{8,9},{9,8},{10,11... | collective-permute-start | bytes 3538952 | tf_op jit(solution)/shard_map/ppermute | solution.py:38
  165.2 27.8 %collective-permute-start.6 = (bf16[128,3072]{1,0:T(8,128)(2,1)}, bf16[128,3072]{1,0:T(8,128)(2,1)S(1)}, u32[]{:S(2)}, u32[]{:S(2)}) collective-permute-start(bf16[128,3072]{1,0:T(8,128)(2,1)} %get-tuple-element.16), channel_id=1, source_target_pairs={{0,2},{2,4},{4,6},{6,0},{1,3},{3,5},{5,7},{7,1},{8,10},{10,12},{12... | collective-permute-start | bytes 2359304 | tf_op jit(solution)/shard_map/ppermute | solution.py:43
  170.8 22.2 %collective-permute-start.7 = (bf16[128,3072]{1,0:T(8,128)(2,1)}, bf16[128,3072]{1,0:T(8,128)(2,1)}, u32[]{:S(2)}, u32[]{:S(2)}) collective-permute-start(bf16[128,3072]{1,0:T(8,128)(2,1)} %get-tuple-element.15), channel_id=1, source_target_pairs={{0,6},{2,0},{4,2},{6,4},{1,7},{3,1},{5,3},{7,5},{8,14},{10,8},{12,... | collective-permute-start | bytes 2359304 | tf_op jit(solution)/shard_map/ppermute | solution.py:43
  181.2 25.5 %collective-permute-start.8 = (bf16[256,256]{1,0:T(8,128)(2,1)}, bf16[256,256]{1,0:T(8,128)(2,1)S(1)}, u32[]{:S(2)}, u32[]{:S(2)}) collective-permute-start(bf16[256,256]{1,0:T(8,128)(2,1)} %get-tuple-element.12.refs_1_), channel_id=1, source_target_pairs={{0,8},{8,0},{1,9},{9,1},{2,10},{10,2},{3,11},{11,3},{4,12},{12,4},... | collective-permute-start | bytes 393224 | tf_op jit(solution)/shard_map/ppermute | solution.py:38
  183.3 25.4 %collective-permute-start.9 = (bf16[256,256]{1,0:T(8,128)(2,1)}, bf16[256,256]{1,0:T(8,128)(2,1)S(1)}, u32[]{:S(2)}, u32[]{:S(2)}) collective-permute-start(bf16[256,256]{1,0:T(8,128)(2,1)} %get-tuple-element.12.refs_1_), channel_id=1, source_target_pairs={{0,4},{4,0},{1,5},{5,1},{2,6},{6,2},{3,7},{7,3},{8,12},{12,8},{9,1... | collective-permute-start | bytes 393224 | tf_op jit(solution)/shard_map/ppermute | solution.py:38
  191.0 17.8 %collective-permute-start.10 = (bf16[256,256]{1,0:T(8,128)(2,1)}, bf16[256,256]{1,0:T(8,128)(2,1)S(1)}, u32[]{:S(2)}, u32[]{:S(2)}) collective-permute-start(bf16[256,256]{1,0:T(8,128)(2,1)} %get-tuple-element.12.refs_1_), channel_id=1, source_target_pairs={{0,12},{4,8},{8,4},{12,0},{1,13},{5,9},{9,5},{13,1},{2,14},{6,10},... | collective-permute-start | bytes 393224 | tf_op jit(solution)/shard_map/ppermute | solution.py:256
  197.9 12.9 %collective-permute-start.12 = (bf16[256,256]{1,0:T(8,128)(2,1)}, bf16[256,256]{1,0:T(8,128)(2,1)S(1)}, u32[]{:S(2)}, u32[]{:S(2)}) collective-permute-start(bf16[256,256]{1,0:T(8,128)(2,1)} %get-tuple-element.13.refs_6_), channel_id=1, source_target_pairs={{0,8},{8,0},{1,9},{9,1},{2,10},{10,2},{3,11},{11,3},{4,12},{12,4},... | collective-permute-start | bytes 393224 | tf_op jit(solution)/shard_map/ppermute | solution.py:38
  201.3 9.5 %collective-permute-start.13 = (bf16[256,256]{1,0:T(8,128)(2,1)}, bf16[256,256]{1,0:T(8,128)(2,1)S(1)}, u32[]{:S(2)}, u32[]{:S(2)}) collective-permute-start(bf16[256,256]{1,0:T(8,128)(2,1)} %get-tuple-element.13.refs_6_), channel_id=1, source_target_pairs={{0,4},{4,0},{1,5},{5,1},{2,6},{6,2},{3,7},{7,3},{8,12},{12,8},{9,1... | collective-permute-start | bytes 393224 | tf_op jit(solution)/shard_map/ppermute | solution.py:38
  206.8 9.5 %collective-permute-start.14 = (bf16[256,256]{1,0:T(8,128)(2,1)}, bf16[256,256]{1,0:T(8,128)(2,1)S(1)}, u32[]{:S(2)}, u32[]{:S(2)}) collective-permute-start(bf16[256,256]{1,0:T(8,128)(2,1)} %get-tuple-element.13.refs_6_), channel_id=1, source_target_pairs={{0,12},{4,8},{8,4},{12,0},{1,13},{5,9},{9,5},{13,1},{2,14},{6,10},... | collective-permute-start | bytes 393224 | tf_op jit(solution)/shard_map/ppermute | solution.py:256
  208.9 12.7 %collective-permute-start.11 = (bf16[1024,256]{1,0:T(8,128)(2,1)S(1)}, bf16[1024,256]{1,0:T(8,128)(2,1)S(1)}, u32[]{:S(2)}, u32[]{:S(2)}) collective-permute-start(bf16[1024,256]{1,0:T(8,128)(2,1)S(1)} %pad_maximum_fusion.2), channel_id=1, source_target_pairs={{0,1},{1,0},{2,3},{3,2},{4,5},{5,4},{6,7},{7,6},{8,9},{9,8},{10,11... | collective-permute-start | bytes 1572872 | tf_op jit(solution)/shard_map/ppermute | solution.py:38
  217.9 3.8 %collective-permute-start.15 = (bf16[1024,256]{1,0:T(8,128)(2,1)S(1)}, bf16[1024,256]{1,0:T(8,128)(2,1)S(1)}, u32[]{:S(2)}, u32[]{:S(2)}) collective-permute-start(bf16[1024,256]{1,0:T(8,128)(2,1)S(1)} %pad_maximum_fusion.3), channel_id=1, source_target_pairs={{0,1},{1,0},{2,3},{3,2},{4,5},{5,4},{6,7},{7,6},{8,9},{9,8},{10,11... | collective-permute-start | bytes 1572872 | tf_op jit(solution)/shard_map/ppermute | solution.py:38
  231.5 33.9 %collective-permute-start.20 = (bf16[384,384]{1,0:T(8,128)(2,1)S(1)}, bf16[384,384]{1,0:T(8,128)(2,1)S(1)}, u32[]{:S(2)}, u32[]{:S(2)}) collective-permute-start(bf16[384,384]{1,0:T(8,128)(2,1)S(1)} %get-tuple-element.18), channel_id=1, source_target_pairs={{0,6},{2,0},{4,2},{6,4},{1,7},{3,1},{5,3},{7,5},{8,14},{10,8},{12,... | collective-permute-start | bytes 884744 | tf_op jit(solution)/shard_map/ppermute | solution.py:43
  234.1 31.4 %collective-permute-start.19 = (bf16[384,384]{1,0:T(8,128)(2,1)S(1)}, bf16[384,384]{1,0:T(8,128)(2,1)S(1)}, u32[]{:S(2)}, u32[]{:S(2)}) collective-permute-start(bf16[384,384]{1,0:T(8,128)(2,1)S(1)} %get-tuple-element.19), channel_id=1, source_target_pairs={{0,4},{2,6},{4,0},{6,2},{1,5},{3,7},{5,1},{7,3},{8,12},{10,14},{12... | collective-permute-start | bytes 884744 | tf_op jit(solution)/shard_map/ppermute | solution.py:43
  237.5 28.0 %collective-permute-start.18 = (bf16[384,384]{1,0:T(8,128)(2,1)S(1)}, bf16[384,384]{1,0:T(8,128)(2,1)S(1)}, u32[]{:S(2)}, u32[]{:S(2)}) collective-permute-start(bf16[384,384]{1,0:T(8,128)(2,1)S(1)} %get-tuple-element.20), channel_id=1, source_target_pairs={{0,2},{2,4},{4,6},{6,0},{1,3},{3,5},{5,7},{7,1},{8,10},{10,12},{12... | collective-permute-start | bytes 884744 | tf_op jit(solution)/shard_map/ppermute | solution.py:43
  240.0 13.6 %collective-permute-start.17 = (bf16[128,128]{1,0:T(8,128)(2,1)S(1)}, bf16[128,128]{1,0:T(8,128)(2,1)S(1)}, u32[]{:S(2)}, u32[]{:S(2)}) collective-permute-start(bf16[128,128]{1,0:T(8,128)(2,1)S(1)} %get-tuple-element.22), channel_id=1, source_target_pairs={{0,2},{2,4},{4,6},{6,0},{1,3},{3,5},{5,7},{7,1},{8,10},{10,12},{12... | collective-permute-start | bytes 98312 | tf_op jit(solution)/shard_map/ppermute | solution.py:43
  244.0 9.6 %collective-permute-start.16 = (bf16[128,128]{1,0:T(8,128)(2,1)S(1)}, bf16[128,128]{1,0:T(8,128)(2,1)S(1)}, u32[]{:S(2)}, u32[]{:S(2)}) collective-permute-start(bf16[128,128]{1,0:T(8,128)(2,1)S(1)} %get-tuple-element.21), channel_id=1, source_target_pairs={{0,6},{2,0},{4,2},{6,4},{1,7},{3,1},{5,3},{7,5},{8,14},{10,8},{12,... | collective-permute-start | bytes 98312 | tf_op jit(solution)/shard_map/ppermute | solution.py:43
  254.4 37.5 %all-to-all-start.1 = ((bf16[16,16,256]{2,1,0:T(8,128)(2,1)}), bf16[16,16,256]{2,1,0:T(8,128)(2,1)S(1)}, u32[]{:S(2)}, u32[]{:S(2)}) async-start(bf16[16,16,256]{2,1,0:T(8,128)(2,1)} %maximum_select_fusion), calls=%async_computation.1 | async-start | bytes 262144 | tf_op jit(solution)/shard_map/all_to_all | solution.py:270
  265.7 57.7 %collective-permute-start.21 = (bf16[4,384,384]{2,1,0:T(8,128)(2,1)S(1)}, bf16[4,384,384]{2,1,0:T(8,128)(2,1)S(1)}, u32[]{:S(2)}, u32[]{:S(2)}) collective-permute-start(bf16[4,384,384]{2,1,0:T(8,128)(2,1)S(1)} %pad_maximum_fusion.1.refs_0_), channel_id=1, source_target_pairs={{0,1},{1,0},{2,3},{3,2},{4,5},{5,4},{6,7},{7,6},{8,9},{9,8},{10,11... | collective-permute-start | bytes 3538952 | tf_op jit(solution)/shard_map/ppermute | solution.py:38
  (21 other events, 204.7 us)
Sparse Core Ops, SparseCore 0:
  10.2 152.2 all-gather.1

commit v2 on v1

--- a/solution.py
+++ b/solution.py
@@ -43,24 +43,20 @@
     return lax.ppermute(value, axes, [(i, (i + shift) % n) for i in range(n)])
 
 
-def modulate_body(tok_ref, scale_ref, shift_ref, rider_ref, out_ref):
+def modulate_body(tok_ref, scale_ref, shift_ref, out_ref):
     values = tok_ref[...].astype(jnp.float32)
-    width = values.shape[1]
     center = jnp.mean(values, axis=-1, keepdims=True)
     spread = jnp.mean(jnp.square(values - center), axis=-1, keepdims=True)
     normed = (values - center) / jnp.sqrt(spread + EPSILON)
-    out_ref[:, :width] = (normed * (1.0 + scale_ref[...]) + shift_ref[...]).astype(jnp.bfloat16)
-    out_ref[:, width:] = rider_ref[...]
-
-
-def modulate(tokens, scale_mod, shift_mod, rider):
+    out_ref[...] = (normed * (1.0 + scale_ref[...]) + shift_ref[...]).astype(jnp.bfloat16)
+
+
+def modulate(tokens, scale_mod, shift_mod):
     return pl.pallas_call(
         modulate_body,
-        out_shape=jax.ShapeDtypeStruct(
-            (tokens.shape[0], tokens.shape[1] + rider.shape[1]), jnp.bfloat16
-        ),
+        out_shape=jax.ShapeDtypeStruct(tokens.shape, jnp.bfloat16),
         name="modulate",
-    )(tokens, scale_mod, shift_mod, rider)
+    )(tokens, scale_mod, shift_mod)
 
 
 def project_body(order_ref, *refs, parts, pieces, head_dim):
@@ -225,10 +221,8 @@
     big, zn, xt, xu, zc = (lax.axis_index(a) for a in ("big", "zn", "xt", "xu", "head"))
     zx = lax.axis_index(INNER)
 
-    rider = out_weight.T.reshape(own, -1)
-    modulated = modulate(tokens.reshape(own, width), scale_mod, shift_mod, rider)
-    gathered = lax.all_gather(modulated, FAR, axis=0, tiled=True)
-    mine = gathered[:, :width]
+    modulated = modulate(tokens.reshape(own, width), scale_mod, shift_mod)
+    mine = lax.all_gather(modulated, FAR, axis=0, tiled=True)
     half = mine.shape[0] // 2
     left = around(mine[:half], INNER, 1)
     right = around(mine[half:], INNER, -1)
@@ -251,16 +245,11 @@
     spot = [(xt ^ t ^ odd_t) + 2 * (zn ^ n) for n, t in ((0, 0), (1, 0), (0, 1), (1, 1))]
     order = jnp.stack([s + 4 * c for c in (zc, 1 - zc) for s in spot]).astype(jnp.int32)
 
-    def exchanged(kv):
-        near = [kv, swapped(kv, "zn"), swapped(kv, "xt")]
-        near.append(lax.ppermute(kv, ("zn", "xt"), [(i, 3 - i) for i in range(4)]))
-        return [*near, swapped(jnp.concatenate(near), "head")]
-
-    query_a, kv_a = project(order, [mine], weights, query_gain, key_gain, head_dim)
-    kvs = exchanged(kv_a)
-    query_b, kv_b = project(order, [left, right], weights, query_gain, key_gain, head_dim)
-    kvs = kvs + exchanged(kv_b)
-    heads_out = attend(jnp.concatenate([query_a, query_b]), kvs, head_dim)
+    query, kv = project(order, [mine, left, right], weights, query_gain, key_gain, head_dim)
+    kvs = [kv, swapped(kv, "zn"), swapped(kv, "xt")]
+    kvs.append(lax.ppermute(kv, ("zn", "xt"), [(i, 3 - i) for i in range(4)]))
+    other = swapped(jnp.concatenate(kvs), "head")
+    heads_out = attend(query, [*kvs, other], head_dim)
 
     ours, to_left, to_right = heads_out[: 2 * half], heads_out[2 * half : 3 * half], heads_out[3 * half :]
     theirs = jnp.concatenate([around(to_left, INNER, -1), around(to_right, INNER, 1)])
@@ -272,14 +261,15 @@
     back = jnp.transpose(back, (2, 0, 1, 3, 4)).reshape(own, sizes[0], -1)[:, :, :local_cols]
     mixed = lax.all_gather(back.reshape(own, width), EIGHT, axis=0, tiled=True)
 
-    out_far, _ = lax.optimization_barrier((gathered[:, width:], heads_out))
-    out_far = out_far.reshape(-1, out_weight.shape[0])
+    out_far = lax.all_gather(out_weight.T, FAR, axis=0, tiled=True)
+    out_far, _ = lax.optimization_barrier((out_far, pair))
     block = out_far.shape[0] // inner
     got = []
     for s in range(inner):
         send = lax.dynamic_slice_in_dim(out_far, (zx + s) % inner * block, block, axis=0)
         got.append((around(send, INNER, s) if s else send)[None])
     outs = jnp.concatenate(got, axis=0)
+    outs, mixed = lax.optimization_barrier((outs, mixed))
     outs = [outs, swapped(outs, "head")]
     source = [(zx - s) % inner * head for s in range(inner)]
     out_order = jnp.stack([s + c for c in (zc, 1 - zc) for s in source]).astype(jnp.int32)

time: 350 us -> 359 us (1.026)
  the two profiles are of different devices: /device:TPU:34 before, /device:TPU:33 now
where the time goes in v2:
time: 359 us; the launch traced here: 358 us
  starting transfers between devices  154 us (43%)
  waiting for transfers between devices  120 us (33%)
  blocking collectives  34.8 us (10%)
  Pallas kernels  18.2 us (5%)
  local copies, waits for them, and re-layouts  14.5 us (4%)
  between operations  13.9 us (4%)
    ppermute x7, starting transfers between devices, swapped(): return lax.ppermute(value, axes, [(i, n - 1 - i) for i in range(n)])  69.5 us
    all_gather x1, waiting for transfers between devices, per_device(): out_far = lax.all_gather(out_weight.T, FAR, axis=0, tiled=True)  38.9 us
    all_gather x1, blocking collectives, per_device(): mixed = lax.all_gather(back.reshape(own, width), EIGHT, axis=0, tiled=True)  25.8 us
    ppermute x1, waiting for transfers between devices, weights_to_tile(): moved = lax.ppermute(moved, GROUP, move)  24.1 us
    ppermute x1, starting transfers between devices, weights_to_tile(): moved = lax.ppermute(moved, GROUP, move)  23.6 us
    ppermute x7, starting transfers between devices, around(): return lax.ppermute(value, axes, [(i, (i + shift) % n) for i in range(n)])  22.4 us
    all_to_all x1, starting transfers between devices, per_device(): lax.all_to_all(pair.reshape(far, own, 2 * head_dim), FAR, 0, 0, tiled=True)  16.1 us
    ppermute x7, waiting for transfers between devices, around(): return lax.ppermute(value, axes, [(i, (i + shift) % n) for i in range(n)])  16 us
  transfers between devices with their start and end apart: 22, of which 14 were waited for; matrix products, arithmetic and copies ran while one was open for 4% of the time, Pallas kernels for 2%

profile of v2, /device:TPU:33, one launch (start us, length us, event | category | flops | bytes accessed | tf_op | source)
XLA Modules:
  0.0 358.0 jit_solution(1572789358282490865)
XLA Ops:
  11.5 23.6 %collective-permute-start.6 = (bf16[3,96,384]{2,1,0:T(8,128)(2,1)S(1)}, bf16[3,96,384]{2,1,0:T(8,128)(2,1)S(1)}, u32[]{:S(2)}, u32[]{:S(2)}) collective-permute-start(bf16[3,96,384]{2,1,0:T(8,128)(2,1)S(1)} %collective-permute-done.5), channel_id=1, source_target_pairs={{0,0},{1,32},{2,66},{3,98},{4,132},{5,164},{6,198},{7,230},{10,2},... | collective-permute-start | bytes 663560 | tf_op jit(solution)/shard_map/ppermute | solution.py:193
  35.2 24.1 %collective-permute-done.6 = bf16[3,96,384]{2,1,0:T(8,128)(2,1)S(1)} collective-permute-done((bf16[3,96,384]{2,1,0:T(8,128)(2,1)S(1)}, bf16[3,96,384]{2,1,0:T(8,128)(2,1)S(1)}, u32[]{:S(2)}, u32[]{:S(2)}) %collective-permute-start.6) | collective-permute-done | bytes 221216 | tf_op jit(solution)/shard_map/ppermute | solution.py:193
  59.9 15.8 %all-to-all-start = ((bf16[4,96,384]{2,1,0:T(8,128)(2,1)}), bf16[4,96,384]{2,1,0:T(8,128)(2,1)S(1)}, u32[]{:S(2)}, u32[]{:S(2)}) async-start(bf16[4,96,384]{2,1,0:T(8,128)(2,1)} %concatenate.40), calls=%async_computation | async-start | bytes 589824 | tf_op jit(solution)/shard_map/all_to_all | solution.py:197
  75.8 13.7 %all-to-all-done = bf16[4,96,384]{2,1,0:T(8,128)(2,1)S(1)} async-done(((bf16[4,96,384]{2,1,0:T(8,128)(2,1)}), bf16[4,96,384]{2,1,0:T(8,128)(2,1)S(1)}, u32[]{:S(2)}, u32[]{:S(2)}) %all-to-all-start) | async-done | bytes 294944 | tf_op jit(solution)/shard_map/all_to_all | solution.py:197
  89.5 14.2 %collective-permute-start.7 = (bf16[1,384,384]{2,1,0:T(8,128)(2,1)S(1)}, bf16[1,384,384]{2,1,0:T(8,128)(2,1)S(1)}, u32[]{:S(2)}, u32[]{:S(2)}) collective-permute-start(bf16[1,384,384]{2,1,0:T(8,128)(2,1)S(1)} %bitcast.47), channel_id=1, source_target_pairs={{0,8},{8,0},{1,9},{9,1},{2,10},{10,2},{3,11},{11,3},{4,12},{12,4},... | collective-permute-start | bytes 884744 | tf_op jit(solution)/shard_map/ppermute | solution.py:38
  103.7 15.4 %collective-permute-start.8 = (bf16[1,384,384]{2,1,0:T(8,128)(2,1)S(1)}, bf16[1,384,384]{2,1,0:T(8,128)(2,1)S(1)}, u32[]{:S(2)}, u32[]{:S(2)}) collective-permute-start(bf16[1,384,384]{2,1,0:T(8,128)(2,1)S(1)} %bitcast.48), channel_id=1, source_target_pairs={{0,4},{4,0},{1,5},{5,1},{2,6},{6,2},{3,7},{7,3},{8,12},{12,8},{9,1... | collective-permute-start | bytes 884744 | tf_op jit(solution)/shard_map/ppermute | solution.py:38
  123.2 10.2 %collective-permute-done.9 = bf16[1,384,384]{2,1,0:T(8,128)(2,1)S(1)} collective-permute-done((bf16[1,384,384]{2,1,0:T(8,128)(2,1)S(1)}, bf16[1,384,384]{2,1,0:T(8,128)(2,1)S(1)}, u32[]{:S(2)}, u32[]{:S(2)}) %collective-permute-start.9) | collective-permute-done | bytes 294944 | tf_op jit(solution)/shard_map/ppermute | solution.py:241
  135.5 6.2 %all-gather.5.cloned.1.call-done.refs_1_ = bf16[256,3072]{1,0:T(8,128)(2,1)} async-done(((bf16[16,3072]{1,0:T(8,128)(2,1)}), bf16[256,3072]{1,0:T(8,128)(2,1)}) %all-gather.5.cloned.1.call-update) | async-done | bytes 1572880 | tf_op jit(solution)/shard_map/all_gather | solution.py:225
  146.3 4.6 %collective-permute-start.4 = (bf16[128,3072]{1,0:T(8,128)(2,1)}, bf16[128,3072]{1,0:T(8,128)(2,1)}, u32[]{:S(2)}, u32[]{:S(2)}) collective-permute-start(bf16[128,3072]{1,0:T(8,128)(2,1)} %get-tuple-element.13), channel_id=1, source_target_pairs={{0,6},{2,0},{4,2},{6,4},{1,7},{3,1},{5,3},{7,5},{8,14},{10,8},{12,... | collective-permute-start | bytes 2359304 | tf_op jit(solution)/shard_map/ppermute | solution.py:43
  151.6 7.7 %collective-permute-done.3.refs_2_ = bf16[128,3072]{1,0:T(8,128)(2,1)S(1)} collective-permute-done((bf16[128,3072]{1,0:T(8,128)(2,1)}, bf16[128,3072]{1,0:T(8,128)(2,1)S(1)}, u32[]{:S(2)}, u32[]{:S(2)}) %collective-permute-start.3) | collective-permute-done | bytes 786464 | tf_op jit(solution)/shard_map/ppermute | solution.py:43
  160.3 5.8 %project.1 = (bf16[512,128]{1,0:T(8,128)(2,1)}, bf16[512,256]{1,0:T(8,128)(2,1)}) custom-call(s32[8]{0:T(128)} %stack.83.refs_0_, bf16[256,3072]{1,0:T(8,128)(2,1)} %all-gather.5.cloned.1.call-done.refs_1_, bf16[128,3072]{1,0:T(8,128)(2,1)} %copy-done.8, bf16[128,3072]{1,0:T(8,128)(2,1)} %collective-permute-done.4.refs_3_, bf16[4,384,384]{2,1,0:T(8,128)(2,1)} %copy-done.1, ...), custom_call_target="tpu_custom_call" | custom-call | tf_op jit(solution)/shard_map/project/pallas_call | solution.py:92
  168.0 4.1 %collective-permute-start.12 = (bf16[512,256]{1,0:T(8,128)(2,1)}, bf16[512,256]{1,0:T(8,128)(2,1)S(1)}, u32[]{:S(2)}, u32[]{:S(2)}) collective-permute-start(bf16[512,256]{1,0:T(8,128)(2,1)} %get-tuple-element.10.refs_1_), channel_id=1, source_target_pairs={{0,4},{4,0},{1,5},{5,1},{2,6},{6,2},{3,7},{7,3},{8,12},{12,8},{9,1... | collective-permute-start | bytes 786440 | tf_op jit(solution)/shard_map/ppermute | solution.py:38
  172.2 3.9 %collective-permute-start.13 = (bf16[512,256]{1,0:T(8,128)(2,1)}, bf16[512,256]{1,0:T(8,128)(2,1)S(1)}, u32[]{:S(2)}, u32[]{:S(2)}) collective-permute-start(bf16[512,256]{1,0:T(8,128)(2,1)} %get-tuple-element.10.refs_1_), channel_id=1, source_target_pairs={{0,12},{4,8},{8,4},{12,0},{1,13},{5,9},{9,5},{13,1},{2,14},{6,10},... | collective-permute-start | bytes 786440 | tf_op jit(solution)/shard_map/ppermute | solution.py:250
  176.9 5.6 %collective-permute-done.13.refs_4_ = bf16[512,256]{1,0:T(8,128)(2,1)S(1)} collective-permute-done((bf16[512,256]{1,0:T(8,128)(2,1)}, bf16[512,256]{1,0:T(8,128)(2,1)S(1)}, u32[]{:S(2)}, u32[]{:S(2)}) %collective-permute-start.13) | collective-permute-done | bytes 262176 | tf_op jit(solution)/shard_map/ppermute | solution.py:250
  183.6 11.3 %collective-permute-start.14 = (bf16[2048,256]{1,0:T(8,128)(2,1)S(1)}, bf16[2048,256]{1,0:T(8,128)(2,1)S(1)}, u32[]{:S(2)}, u32[]{:S(2)}) collective-permute-start(bf16[2048,256]{1,0:T(8,128)(2,1)S(1)} %pad_maximum_fusion.2), channel_id=1, source_target_pairs={{0,1},{1,0},{2,3},{3,2},{4,5},{5,4},{6,7},{7,6},{8,9},{9,8},{10,11... | collective-permute-start | bytes 3145736 | tf_op jit(solution)/shard_map/ppermute | solution.py:38
  198.1 7.2 %attend.1 = bf16[512,128]{1,0:T(8,128)(2,1)} custom-call(bf16[512,128]{1,0:T(8,128)(2,1)} %get-tuple-element.9.refs_0_, bf16[512,256]{1,0:T(8,128)(2,1)} %get-tuple-element.10.refs_1_, bf16[512,256]{1,0:T(8,128)(2,1)} %copy-done.5, bf16[512,256]{1,0:T(8,128)(2,1)} %copy-done.6, bf16[512,256]{1,0:T(8,128)(2,1)} %copy-done.7, bf16[2048,256]{1,0:T(8,128)(2,1)} %copy-done.4), custom_call_target="tpu_custom_call" | custom-call | tf_op jit(solution)/shard_map/attend/pallas_call | solution.py:143
  206.1 3.7 %collective-permute-start.15 = (bf16[128,128]{1,0:T(8,128)(2,1)S(1)}, bf16[128,128]{1,0:T(8,128)(2,1)S(1)}, u32[]{:S(2)}, u32[]{:S(2)}) collective-permute-start(bf16[128,128]{1,0:T(8,128)(2,1)S(1)} %get-tuple-element.19), channel_id=1, source_target_pairs={{0,6},{2,0},{4,2},{6,4},{1,7},{3,1},{5,3},{7,5},{8,14},{10,8},{12,... | collective-permute-start | bytes 98312 | tf_op jit(solution)/shard_map/ppermute | solution.py:43
  216.4 16.1 %all-to-all-start.1 = ((bf16[16,16,256]{2,1,0:T(8,128)(2,1)}), bf16[16,16,256]{2,1,0:T(8,128)(2,1)S(1)}, u32[]{:S(2)}, u32[]{:S(2)}) async-start(bf16[16,16,256]{2,1,0:T(8,128)(2,1)} %maximum_select_fusion), calls=%async_computation.1 | async-start | bytes 262144 | tf_op jit(solution)/shard_map/all_to_all | solution.py:259
  232.5 38.9 %all-gather.3.cloned.1.call-done = bf16[1536,384]{1,0:T(8,128)(2,1)} async-done(((bf16[96,384]{1,0:T(8,128)(2,1)}), bf16[1536,384]{1,0:T(8,128)(2,1)}) %all-gather.3.cloned.1.call-update) | async-done | bytes 1179664 | tf_op jit(solution)/shard_map/all_gather | solution.py:264
  275.2 3.4 collective-permute-start.1
  278.7 4.0 %collective-permute-start.2 = (bf16[384,384]{1,0:T(8,128)(2,1)S(1)}, bf16[384,384]{1,0:T(8,128)(2,1)S(1)}, u32[]{:S(2)}, u32[]{:S(2)}) collective-permute-start(bf16[384,384]{1,0:T(8,128)(2,1)S(1)} %get-tuple-element.16), channel_id=1, source_target_pairs={{0,6},{2,0},{4,2},{6,4},{1,7},{3,1},{5,3},{7,5},{8,14},{10,8},{12,... | collective-permute-start | bytes 884744 | tf_op jit(solution)/shard_map/ppermute | solution.py:43
  287.6 25.8 %all_gather.11.mixed_ref = bf16[128,3072]{1,0:T(8,128)(2,1)} all-gather(bf16[16,3072]{1,0:T(8,128)(2,1)S(1)} %bitcast.56), channel_id=1, replica_groups=mesh['clip'=2,'big'=8,'zh'=2,'zn'=2,'xt'=2,'xu'=2,'head'=2] {'zn','xt','..., dimensions={0}, use_global_device_ids=true | all-gather | bytes 884736 | tf_op jit(solution)/shard_map/all_gather | solution.py:262
  313.3 20.6 %collective-permute-start.17 = (bf16[4,384,384]{2,1,0:T(8,128)(2,1)S(1)}, bf16[4,384,384]{2,1,0:T(8,128)(2,1)S(1)}, u32[]{:S(2)}, u32[]{:S(2)}) collective-permute-start(bf16[4,384,384]{2,1,0:T(8,128)(2,1)S(1)} %pad_maximum_fusion.refs_0_), channel_id=1, source_target_pairs={{0,1},{1,0},{2,3},{3,2},{4,5},{5,4},{6,7},{7,6},{8,9},{9,8},{10,11... | collective-permute-start | bytes 3538952 | tf_op jit(solution)/shard_map/ppermute | solution.py:38
  341.0 9.0 %all_to_all.15 = bf16[8,16,384]{2,1,0:T(8,128)(2,1)S(1)} all-to-all(bf16[8,16,384]{2,1,0:T(8,128)(2,1)} %bitcast.54), channel_id=1, replica_groups=mesh['clip'=2,'big'=8,'zh'=2,'zn'=2,'xt'=2,'xu'=2,'head'=2] {'zn','xt','..., dimensions={0} | all-to-all | bytes 196608 | tf_op jit(solution)/shard_map/all_to_all | solution.py:280
  (79 shorter events, 49.4 us)
Async XLA Ops:
  6.5 135.2 %all-gather.5.cloned.1.call-start = ((), (), s32[]{:S(2)}) async-start(), calls=%async_computation.4 | async-start | bytes 1671168 | tf_op jit(solution)/shard_map/all_gather | solution.py:225
  10.8 0.7 collective-permute-start.5
  11.5 47.7 %collective-permute-start.6 = (bf16[3,96,384]{2,1,0:T(8,128)(2,1)S(1)}, bf16[3,96,384]{2,1,0:T(8,128)(2,1)S(1)}, u32[]{:S(2)}, u32[]{:S(2)}) collective-permute-start(bf16[3,96,384]{2,1,0:T(8,128)(2,1)S(1)} %collective-permute-done.5), channel_id=1, source_target_pairs={{0,0},{1,32},{2,66},{3,98},{4,132},{5,164},{6,198},{7,230},{10,2},... | collective-permute-start | bytes 663560 | tf_op jit(solution)/shard_map/ppermute | solution.py:193
  59.9 29.5 %all-to-all-start = ((bf16[4,96,384]{2,1,0:T(8,128)(2,1)}), bf16[4,96,384]{2,1,0:T(8,128)(2,1)S(1)}, u32[]{:S(2)}, u32[]{:S(2)}) async-start(bf16[4,96,384]{2,1,0:T(8,128)(2,1)} %concatenate.40), calls=%async_computation | async-start | bytes 589824 | tf_op jit(solution)/shard_map/all_to_all | solution.py:197
  75.7 195.6 %all-gather.3.cloned.1.call-start = ((), (), s32[]{:S(2)}) async-start(), calls=%async_computation.3 | async-start | bytes 1253376 | tf_op jit(solution)/shard_map/all_gather | solution.py:264
  89.5 31.6 %collective-permute-start.7 = (bf16[1,384,384]{2,1,0:T(8,128)(2,1)S(1)}, bf16[1,384,384]{2,1,0:T(8,128)(2,1)S(1)}, u32[]{:S(2)}, u32[]{:S(2)}) collective-permute-start(bf16[1,384,384]{2,1,0:T(8,128)(2,1)S(1)} %bitcast.47), channel_id=1, source_target_pairs={{0,8},{8,0},{1,9},{9,1},{2,10},{10,2},{3,11},{11,3},{4,12},{12,4},... | collective-permute-start | bytes 884744 | tf_op jit(solution)/shard_map/ppermute | solution.py:38
  103.7 19.5 %collective-permute-start.8 = (bf16[1,384,384]{2,1,0:T(8,128)(2,1)S(1)}, bf16[1,384,384]{2,1,0:T(8,128)(2,1)S(1)}, u32[]{:S(2)}, u32[]{:S(2)}) collective-permute-start(bf16[1,384,384]{2,1,0:T(8,128)(2,1)S(1)} %bitcast.48), channel_id=1, source_target_pairs={{0,4},{4,0},{1,5},{5,1},{2,6},{6,2},{3,7},{7,3},{8,12},{12,8},{9,1... | collective-permute-start | bytes 884744 | tf_op jit(solution)/shard_map/ppermute | solution.py:38
  119.1 14.3 %collective-permute-start.9 = (bf16[1,384,384]{2,1,0:T(8,128)(2,1)S(1)}, bf16[1,384,384]{2,1,0:T(8,128)(2,1)S(1)}, u32[]{:S(2)}, u32[]{:S(2)}) collective-permute-start(bf16[1,384,384]{2,1,0:T(8,128)(2,1)S(1)} %bitcast.49), channel_id=1, source_target_pairs={{0,12},{4,8},{8,4},{12,0},{1,13},{5,9},{9,5},{13,1},{2,14},{6,10},... | collective-permute-start | bytes 884744 | tf_op jit(solution)/shard_map/ppermute | solution.py:241
  133.6 18.0 %collective-permute-start.10 = (bf16[4,384,384]{2,1,0:T(8,128)(2,1)S(1)}, bf16[4,384,384]{2,1,0:T(8,128)(2,1)S(1)}, u32[]{:S(2)}, u32[]{:S(2)}) collective-permute-start(bf16[4,384,384]{2,1,0:T(8,128)(2,1)S(1)} %pad_maximum_fusion.1.refs_4_), channel_id=1, source_target_pairs={{0,1},{1,0},{2,3},{3,2},{4,5},{5,4},{6,7},{7,6},{8,9},{9,8},{10,11... | collective-permute-start | bytes 3538952 | tf_op jit(solution)/shard_map/ppermute | solution.py:38
  144.4 14.9 %collective-permute-start.3 = (bf16[128,3072]{1,0:T(8,128)(2,1)}, bf16[128,3072]{1,0:T(8,128)(2,1)S(1)}, u32[]{:S(2)}, u32[]{:S(2)}) collective-permute-start(bf16[128,3072]{1,0:T(8,128)(2,1)} %get-tuple-element.14), channel_id=1, source_target_pairs={{0,2},{2,4},{4,6},{6,0},{1,3},{3,5},{5,7},{7,1},{8,10},{10,12},{12... | collective-permute-start | bytes 2359304 | tf_op jit(solution)/shard_map/ppermute | solution.py:43
  146.3 14.0 %collective-permute-start.4 = (bf16[128,3072]{1,0:T(8,128)(2,1)}, bf16[128,3072]{1,0:T(8,128)(2,1)}, u32[]{:S(2)}, u32[]{:S(2)}) collective-permute-start(bf16[128,3072]{1,0:T(8,128)(2,1)} %get-tuple-element.13), channel_id=1, source_target_pairs={{0,6},{2,0},{4,2},{6,4},{1,7},{3,1},{5,3},{7,5},{8,14},{10,8},{12,... | collective-permute-start | bytes 2359304 | tf_op jit(solution)/shard_map/ppermute | solution.py:43
  166.1 10.0 %collective-permute-start.11 = (bf16[512,256]{1,0:T(8,128)(2,1)}, bf16[512,256]{1,0:T(8,128)(2,1)S(1)}, u32[]{:S(2)}, u32[]{:S(2)}) collective-permute-start(bf16[512,256]{1,0:T(8,128)(2,1)} %get-tuple-element.10.refs_1_), channel_id=1, source_target_pairs={{0,8},{8,0},{1,9},{9,1},{2,10},{10,2},{3,11},{11,3},{4,12},{12,4},... | collective-permute-start | bytes 786440 | tf_op jit(solution)/shard_map/ppermute | solution.py:38
  168.0 8.9 %collective-permute-start.12 = (bf16[512,256]{1,0:T(8,128)(2,1)}, bf16[512,256]{1,0:T(8,128)(2,1)S(1)}, u32[]{:S(2)}, u32[]{:S(2)}) collective-permute-start(bf16[512,256]{1,0:T(8,128)(2,1)} %get-tuple-element.10.refs_1_), channel_id=1, source_target_pairs={{0,4},{4,0},{1,5},{5,1},{2,6},{6,2},{3,7},{7,3},{8,12},{12,8},{9,1... | collective-permute-start | bytes 786440 | tf_op jit(solution)/shard_map/ppermute | solution.py:38
  172.2 10.3 %collective-permute-start.13 = (bf16[512,256]{1,0:T(8,128)(2,1)}, bf16[512,256]{1,0:T(8,128)(2,1)S(1)}, u32[]{:S(2)}, u32[]{:S(2)}) collective-permute-start(bf16[512,256]{1,0:T(8,128)(2,1)} %get-tuple-element.10.refs_1_), channel_id=1, source_target_pairs={{0,12},{4,8},{8,4},{12,0},{1,13},{5,9},{9,5},{13,1},{2,14},{6,10},... | collective-permute-start | bytes 786440 | tf_op jit(solution)/shard_map/ppermute | solution.py:250
  183.6 13.5 %collective-permute-start.14 = (bf16[2048,256]{1,0:T(8,128)(2,1)S(1)}, bf16[2048,256]{1,0:T(8,128)(2,1)S(1)}, u32[]{:S(2)}, u32[]{:S(2)}) collective-permute-start(bf16[2048,256]{1,0:T(8,128)(2,1)S(1)} %pad_maximum_fusion.2), channel_id=1, source_target_pairs={{0,1},{1,0},{2,3},{3,2},{4,5},{5,4},{6,7},{7,6},{8,9},{9,8},{10,11... | collective-permute-start | bytes 3145736 | tf_op jit(solution)/shard_map/ppermute | solution.py:38
  206.1 6.8 %collective-permute-start.15 = (bf16[128,128]{1,0:T(8,128)(2,1)S(1)}, bf16[128,128]{1,0:T(8,128)(2,1)S(1)}, u32[]{:S(2)}, u32[]{:S(2)}) collective-permute-start(bf16[128,128]{1,0:T(8,128)(2,1)S(1)} %get-tuple-element.19), channel_id=1, source_target_pairs={{0,6},{2,0},{4,2},{6,4},{1,7},{3,1},{5,3},{7,5},{8,14},{10,8},{12,... | collective-permute-start | bytes 98312 | tf_op jit(solution)/shard_map/ppermute | solution.py:43
  209.8 5.9 %collective-permute-start.16 = (bf16[128,128]{1,0:T(8,128)(2,1)S(1)}, bf16[128,128]{1,0:T(8,128)(2,1)S(1)}, u32[]{:S(2)}, u32[]{:S(2)}) collective-permute-start(bf16[128,128]{1,0:T(8,128)(2,1)S(1)} %get-tuple-element.20), channel_id=1, source_target_pairs={{0,2},{2,4},{4,6},{6,0},{1,3},{3,5},{5,7},{7,1},{8,10},{10,12},{12... | collective-permute-start | bytes 98312 | tf_op jit(solution)/shard_map/ppermute | solution.py:43
  216.4 71.0 %all-to-all-start.1 = ((bf16[16,16,256]{2,1,0:T(8,128)(2,1)}), bf16[16,16,256]{2,1,0:T(8,128)(2,1)S(1)}, u32[]{:S(2)}, u32[]{:S(2)}) async-start(bf16[16,16,256]{2,1,0:T(8,128)(2,1)} %maximum_select_fusion), calls=%async_computation.1 | async-start | bytes 262144 | tf_op jit(solution)/shard_map/all_to_all | solution.py:259
  272.7 11.9 %collective-permute-start = (bf16[384,384]{1,0:T(8,128)(2,1)S(1)}, bf16[384,384]{1,0:T(8,128)(2,1)S(1)}, u32[]{:S(2)}, u32[]{:S(2)}) collective-permute-start(bf16[384,384]{1,0:T(8,128)(2,1)S(1)} %get-tuple-element.18), channel_id=1, source_target_pairs={{0,2},{2,4},{4,6},{6,0},{1,3},{3,5},{5,7},{7,1},{8,10},{10,12},{12... | collective-permute-start | bytes 884744 | tf_op jit(solution)/shard_map/ppermute | solution.py:43
  275.2 9.3 %collective-permute-start.1 = (bf16[384,384]{1,0:T(8,128)(2,1)S(1)}, bf16[384,384]{1,0:T(8,128)(2,1)S(1)}, u32[]{:S(2)}, u32[]{:S(2)}) collective-permute-start(bf16[384,384]{1,0:T(8,128)(2,1)S(1)} %get-tuple-element.17), channel_id=1, source_target_pairs={{0,4},{2,6},{4,0},{6,2},{1,5},{3,7},{5,1},{7,3},{8,12},{10,14},{12... | collective-permute-start | bytes 884744 | tf_op jit(solution)/shard_map/ppermute | solution.py:43
  278.7 8.4 %collective-permute-start.2 = (bf16[384,384]{1,0:T(8,128)(2,1)S(1)}, bf16[384,384]{1,0:T(8,128)(2,1)S(1)}, u32[]{:S(2)}, u32[]{:S(2)}) collective-permute-start(bf16[384,384]{1,0:T(8,128)(2,1)S(1)} %get-tuple-element.16), channel_id=1, source_target_pairs={{0,6},{2,0},{4,2},{6,4},{1,7},{3,1},{5,3},{7,5},{8,14},{10,8},{12,... | collective-permute-start | bytes 884744 | tf_op jit(solution)/shard_map/ppermute | solution.py:43
  287.3 49.3 %copy-start = (bf16[4,384,384]{2,1,0:T(8,128)(2,1)}, bf16[4,384,384]{2,1,0:T(8,128)(2,1)S(1)}, u32[]{:S(2)}) copy-start(bf16[4,384,384]{2,1,0:T(8,128)(2,1)S(1)} %pad_maximum_fusion.refs_0_) | copy-start | bytes 3538948
  287.3 47.3 %copy-start.9 = (f32[1,3072]{1,0:T(1,128)S(1)}, f32[1,3072]{1,0:T(1,128)}, u32[]{:S(2)}) copy-start(f32[1,3072]{1,0:T(1,128)} %param.13) | copy-start | bytes 36868
  313.3 23.2 %collective-permute-start.17 = (bf16[4,384,384]{2,1,0:T(8,128)(2,1)S(1)}, bf16[4,384,384]{2,1,0:T(8,128)(2,1)S(1)}, u32[]{:S(2)}, u32[]{:S(2)}) collective-permute-start(bf16[4,384,384]{2,1,0:T(8,128)(2,1)S(1)} %pad_maximum_fusion.refs_0_), channel_id=1, source_target_pairs={{0,1},{1,0},{2,3},{3,2},{4,5},{5,4},{6,7},{7,6},{8,9},{9,8},{10,11... | collective-permute-start | bytes 3538952 | tf_op jit(solution)/shard_map/ppermute | solution.py:38
  (8 other events, 78.5 us)
Sparse Core Ops, SparseCore 0:
  9.4 132.2 all-gather.4
  176.2 95.0 all-gather.2

commit v3 on v2

--- a/solution.py
+++ b/solution.py
@@ -59,7 +59,7 @@
     )(tokens, scale_mod, shift_mod)
 
 
-def project_body(order_ref, *refs, parts, pieces, head_dim):
+def project_body(place_ref, *refs, parts, pieces, head_dim):
     toks, w_refs = refs[:parts], refs[parts : parts + pieces]
     qg_ref, kg_ref, q_ref, kv_ref = refs[parts + pieces :]
     depth = w_refs[0].shape[-2]
@@ -73,7 +73,7 @@
         acc, k = None, 0
         for w_ref in w_refs:
             for s in range(w_ref.shape[0]):
-                start = pl.multiple_of(order_ref[k] * depth, 128)
+                start = pl.multiple_of((place_ref[0] ^ k) * depth, 128)
                 term = jnp.dot(
                     tok[:, pl.ds(start, depth)], w_ref[s], preferred_element_type=jnp.float32
                 )
@@ -85,7 +85,7 @@
         row += tok.shape[0]
 
 
-def project(order, toks, weights, query_gain, key_gain, head_dim):
+def project(place, toks, weights, query_gain, key_gain, head_dim):
     rows = sum(t.shape[0] for t in toks)
     vmem = pl.BlockSpec(memory_space=pltpu.VMEM)
     smem = pl.BlockSpec(memory_space=pltpu.SMEM)
@@ -99,7 +99,7 @@
             jax.ShapeDtypeStruct((rows, 2 * head_dim), jnp.bfloat16),
         ),
         name="project",
-    )(order, *toks, *weights, query_gain[None], key_gain[None])
+    )(place, *toks, *weights, query_gain[None], key_gain[None])
 
 
 def attend_body(q_ref, *refs, head_dim, chunk):
@@ -136,48 +136,54 @@
     out_ref[...] = (acc / total).astype(jnp.bfloat16)
 
 
-def attend(query, kvs, head_dim):
-    rows = 128
+def attend(query, kvs, head_dim, first, last):
+    rows = 256
     keys = sum(kv.shape[0] for kv in kvs)
     whole = [pl.BlockSpec(kv.shape, lambda i: (0, 0)) for kv in kvs]
     return pl.pallas_call(
         lambda *refs: attend_body(*refs, head_dim=head_dim, chunk=512),
-        grid=(query.shape[0] // rows,),
-        in_specs=[pl.BlockSpec((rows, head_dim), lambda i: (i, 0))] + whole,
+        grid=((last - first) // rows,),
+        in_specs=[pl.BlockSpec((rows, head_dim), lambda i: (i + first // rows, 0))] + whole,
         out_specs=pl.BlockSpec((rows, head_dim), lambda i: (i, 0)),
         scratch_shapes=[pltpu.VMEM((rows, keys), jnp.float32)],
-        out_shape=jax.ShapeDtypeStruct(query.shape, jnp.bfloat16),
+        out_shape=jax.ShapeDtypeStruct((last - first, head_dim), jnp.bfloat16),
         name="attend",
     )(query, *kvs)
 
 
-def combine_body(order_ref, mixed_ref, *refs):
+def combine_body(place_ref, mixed_ref, *refs, head, inner):
     *w_refs, gate_ref, out_ref = refs
-    summed, k = None, 0
-    for w_ref in w_refs:
+    zx, zc, zn = place_ref[0] // (2 * head), place_ref[0] // 2 % head, place_ref[0] % 2
+    summed = None
+    for side, w_ref in enumerate(w_refs):
         depth = w_ref.shape[-1]
         for s in range(w_ref.shape[0]):
-            start = pl.multiple_of(order_ref[k] * depth, 128)
+            group = (zx + inner - s) % inner * head + (zc ^ side)
             term = lax.dot_general(
-                mixed_ref[:, pl.ds(start, depth)],
+                mixed_ref[:, pl.ds(pl.multiple_of(group * depth, 128), depth)],
                 w_ref[s],
                 (((1,), (1,)), ((), ())),
                 preferred_element_type=jnp.float32,
             )
             term = term.astype(jnp.bfloat16).astype(jnp.float32)
-            summed, k = term if summed is None else summed + term, k + 1
-    out_ref[...] = (summed * gate_ref[...]).astype(jnp.bfloat16)
-
-
-def combine(order, mixed, weights, gate):
+            summed = term if summed is None else summed + term
+    step = gate_ref.shape[1]
+    parts = out_ref.shape[1] // step
+    for f in range(parts):
+        gate = gate_ref[pl.ds(2 * (zx * parts + f) + zn, 1), :]
+        cols = slice(f * step, (f + 1) * step)
+        out_ref[:, cols] = (summed[:, cols] * gate).astype(jnp.bfloat16)
+
+
+def combine(place, mixed, weights, gate, head, inner):
     vmem = pl.BlockSpec(memory_space=pltpu.VMEM)
     smem = pl.BlockSpec(memory_space=pltpu.SMEM)
     return pl.pallas_call(
-        combine_body,
+        lambda *refs: combine_body(*refs, head=head, inner=inner),
         in_specs=[smem] + [vmem] * (len(weights) + 2),
-        out_shape=jax.ShapeDtypeStruct((mixed.shape[0], gate.shape[1]), jnp.bfloat16),
+        out_shape=jax.ShapeDtypeStruct((mixed.shape[0], weights[0].shape[1]), jnp.bfloat16),
         name="combine",
-    )(order, mixed, *weights, gate)
+    )(place, mixed, *weights, gate)
 
 
 def weights_to_tile(packed, sizes):
@@ -237,29 +243,29 @@
         ]
     )
     piece = weights_to_tile(packed, sizes)
-    near = [piece, swapped(piece, "zn"), swapped(piece, "xt"), None]
+    near = [piece, swapped(piece, "xt"), swapped(piece, "zn"), None]
     near[3] = lax.ppermute(piece, ("zn", "xt"), [(i, 3 - i) for i in range(4)])
     stack = jnp.concatenate(near, axis=0)
     weights = [stack, swapped(stack, "head")]
     odd_t = big // (2 * head)
-    spot = [(xt ^ t ^ odd_t) + 2 * (zn ^ n) for n, t in ((0, 0), (1, 0), (0, 1), (1, 1))]
-    order = jnp.stack([s + 4 * c for c in (zc, 1 - zc) for s in spot]).astype(jnp.int32)
-
-    query, kv = project(order, [mine, left, right], weights, query_gain, key_gain, head_dim)
-    kvs = [kv, swapped(kv, "zn"), swapped(kv, "xt")]
-    kvs.append(lax.ppermute(kv, ("zn", "xt"), [(i, 3 - i) for i in range(4)]))
-    other = swapped(jnp.concatenate(kvs), "head")
-    heads_out = attend(query, [*kvs, other], head_dim)
-
-    ours, to_left, to_right = heads_out[: 2 * half], heads_out[2 * half : 3 * half], heads_out[3 * half :]
-    theirs = jnp.concatenate([around(to_left, INNER, -1), around(to_right, INNER, 1)])
+    place = ((xt ^ odd_t) + 2 * zn + 4 * zc).astype(jnp.int32).reshape(1)
+
+    query, kv = project(place, [mine, left, right], weights, query_gain, key_gain, head_dim)
+    near = jnp.broadcast_to(kv, (lax.axis_size(("zn", "xt")), *kv.shape))
+    near = lax.all_to_all(near, ("zn", "xt"), 0, 0, tiled=True).reshape(-1, kv.shape[1])
+    kvs = [near, swapped(near, "head")]
+    away = attend(query, kvs, head_dim, 2 * half, 4 * half)
+    theirs = [around(away[:half], INNER, -1), around(away[half:], INNER, 1)]
+    ours = attend(query, kvs, head_dim, 0, 2 * half)
+    theirs = jnp.concatenate(theirs)
     pair = jnp.where(
         xu == 0, jnp.concatenate([ours, theirs], axis=1), jnp.concatenate([theirs, ours], axis=1)
     )
     back = lax.all_to_all(pair.reshape(far, own, 2 * head_dim), FAR, 0, 0, tiled=True)
     back = back.reshape(sizes[0], sizes[1], own, 2, head_dim)
     back = jnp.transpose(back, (2, 0, 1, 3, 4)).reshape(own, sizes[0], -1)[:, :, :local_cols]
-    mixed = lax.all_gather(back.reshape(own, width), EIGHT, axis=0, tiled=True)
+    copies = jnp.broadcast_to(back.reshape(own, width), (lax.axis_size(EIGHT), own, width))
+    mixed = lax.all_to_all(copies, EIGHT, 0, 0, tiled=True).reshape(-1, width)
 
     out_far = lax.all_gather(out_weight.T, FAR, axis=0, tiled=True)
     out_far, _ = lax.optimization_barrier((out_far, pair))
@@ -269,14 +275,10 @@
         send = lax.dynamic_slice_in_dim(out_far, (zx + s) % inner * block, block, axis=0)
         got.append((around(send, INNER, s) if s else send)[None])
     outs = jnp.concatenate(got, axis=0)
-    outs, mixed = lax.optimization_barrier((outs, mixed))
     outs = [outs, swapped(outs, "head")]
-    source = [(zx - s) % inner * head for s in range(inner)]
-    out_order = jnp.stack([s + c for c in (zc, 1 - zc) for s in source]).astype(jnp.int32)
-    gate = gate_mod.reshape(inner, far // inner, sizes[2], -1)
-    gate = lax.dynamic_index_in_dim(gate, zx, 0, keepdims=False)
-    gate = lax.dynamic_index_in_dim(gate, zn, 1, keepdims=False).reshape(1, block)
-    done = combine(out_order, mixed, outs, gate)
+    here = ((zx * head + zc) * 2 + zn).astype(jnp.int32).reshape(1)
+    gate = gate_mod.reshape(far * sizes[2], -1)
+    done = combine(here, mixed, outs, gate, head, inner)
     done = lax.all_to_all(done.reshape(-1, own, block), EIGHT, 0, 0, tiled=True)
     done = done.reshape(sizes[2], inner, own, far // inner, -1)
     return jnp.transpose(done, (2, 1, 3, 0, 4)).reshape(clips, own, width)

time: 359 us -> 391 us (1.089)
  waiting for transfers between devices: 120 us -> 158 us
  starting transfers between devices: 154 us -> 124 us
  blocking collectives: 34.8 us -> 58.5 us
    all_to_all x0 -> x2, blocking collectives: none -> 49.7 us  [the longest x1 35.4 us: per_device(): lax.all_to_all(pair.reshape(far, own, 2 * head_dim), FAR, 0, 0, tiled=True)]
    all_gather x1, waiting for transfers between devices: 38.9 us -> 79.5 us  [per_device(): out_far = lax.all_gather(out_weight.T, FAR, axis=0, tiled=True)]
    ppermute x7 -> x5, starting transfers between devices: 69.5 us -> 30.6 us  [swapped(): return lax.ppermute(value, axes, [(i, n - 1 - i) for i in range(n)])]
    all_gather x1 -> x0, blocking collectives: 25.8 us -> none  [per_device(): mixed = lax.all_gather(back.reshape(own, width), EIGHT, axis=0, tiled=True)]
    ppermute x1, starting transfers between devices: 1.95 us -> 26.2 us  [per_device(): near[3] = lax.ppermute(piece, ('zn', 'xt'), [(i, 3 - i) for i in range(4)])]
    all_to_all x1, starting transfers between devices: 16.1 us -> 3.75 us  [per_device(): mixed = lax.all_to_all(copies, EIGHT, 0, 0, tiled=True).reshape(-1, width)]
    all_gather x1, waiting for transfers between devices: 6.18 us -> 12 us  [per_device(): mine = lax.all_gather(modulated, FAR, axis=0, tiled=True)]
    ppermute x1, waiting for transfers between devices: 10.2 us -> 4.54 us  [per_device(): near[3] = lax.ppermute(piece, ('zn', 'xt'), [(i, 3 - i) for i in range(4)])]
  transfers between devices with their start and end apart: 22 -> 19, of which waited for: 14 -> 12; matrix products, arithmetic and copies ran while one was open for 4% -> 2% of each run, Pallas kernels for 2% -> 1%
where the time goes in v3:
time: 391 us; the launch traced here: 390 us
  waiting for transfers between devices  158 us (40%)
  starting transfers between devices  124 us (32%)
  blocking collectives  58.5 us (15%)
  Pallas kernels  19.4 us (5%)
  local copies, waits for them, and re-layouts  14.6 us (4%)
  between operations  13.8 us (4%)
    all_gather x1, waiting for transfers between devices, per_device(): out_far = lax.all_gather(out_weight.T, FAR, axis=0, tiled=True)  79.5 us
    all_to_all x1, blocking collectives, per_device(): lax.all_to_all(pair.reshape(far, own, 2 * head_dim), FAR, 0, 0, tiled=True)  35.4 us
    ppermute x5, starting transfers between devices, swapped(): return lax.ppermute(value, axes, [(i, n - 1 - i) for i in range(n)])  30.6 us
    ppermute x1, starting transfers between devices, per_device(): near[3] = lax.ppermute(piece, ('zn', 'xt'), [(i, 3 - i) for i in range(4)])  26.2 us
    ppermute x1, waiting for transfers between devices, weights_to_tile(): moved = lax.ppermute(moved, GROUP, move)  24.1 us
    ppermute x1, starting transfers between devices, weights_to_tile(): moved = lax.ppermute(moved, GROUP, move)  23.6 us
    ppermute x7, starting transfers between devices, around(): return lax.ppermute(value, axes, [(i, (i + shift) % n) for i in range(n)])  23 us
    ppermute x7, waiting for transfers between devices, around(): return lax.ppermute(value, axes, [(i, (i + shift) % n) for i in range(n)])  16.5 us
  transfers between devices with their start and end apart: 19, of which 12 were waited for; matrix products, arithmetic and copies ran while one was open for 2% of the time, Pallas kernels for 1%

profile of v3, /device:TPU:33, one launch (start us, length us, event | category | flops | bytes accessed | tf_op | source)
XLA Modules:
  0.0 389.7 jit_solution(17465029341093988518)
XLA Ops:
  11.5 23.6 %collective-permute-start.3 = (bf16[3,96,384]{2,1,0:T(8,128)(2,1)S(1)}, bf16[3,96,384]{2,1,0:T(8,128)(2,1)S(1)}, u32[]{:S(2)}, u32[]{:S(2)}) collective-permute-start(bf16[3,96,384]{2,1,0:T(8,128)(2,1)S(1)} %collective-permute-done.2), channel_id=1, source_target_pairs={{0,0},{1,32},{2,66},{3,98},{4,132},{5,164},{6,198},{7,230},{10,2},... | collective-permute-start | bytes 663560 | tf_op jit(solution)/shard_map/ppermute | solution.py:199
  35.2 24.1 %collective-permute-done.3 = bf16[3,96,384]{2,1,0:T(8,128)(2,1)S(1)} collective-permute-done((bf16[3,96,384]{2,1,0:T(8,128)(2,1)S(1)}, bf16[3,96,384]{2,1,0:T(8,128)(2,1)S(1)}, u32[]{:S(2)}, u32[]{:S(2)}) %collective-permute-start.3) | collective-permute-done | bytes 221216 | tf_op jit(solution)/shard_map/ppermute | solution.py:199
  60.0 15.8 %all-to-all-start = ((bf16[4,96,384]{2,1,0:T(8,128)(2,1)}), bf16[4,96,384]{2,1,0:T(8,128)(2,1)S(1)}, u32[]{:S(2)}, u32[]{:S(2)}) async-start(bf16[4,96,384]{2,1,0:T(8,128)(2,1)} %concatenate.36), calls=%async_computation | async-start | bytes 589824 | tf_op jit(solution)/shard_map/all_to_all | solution.py:203
  75.8 13.7 %all-to-all-done = bf16[4,96,384]{2,1,0:T(8,128)(2,1)S(1)} async-done(((bf16[4,96,384]{2,1,0:T(8,128)(2,1)}), bf16[4,96,384]{2,1,0:T(8,128)(2,1)S(1)}, u32[]{:S(2)}, u32[]{:S(2)}) %all-to-all-start) | async-done | bytes 294944 | tf_op jit(solution)/shard_map/all_to_all | solution.py:203
  89.5 26.2 %collective-permute-start.6 = (bf16[1,384,384]{2,1,0:T(8,128)(2,1)S(1)}, bf16[1,384,384]{2,1,0:T(8,128)(2,1)S(1)}, u32[]{:S(2)}, u32[]{:S(2)}) collective-permute-start(bf16[1,384,384]{2,1,0:T(8,128)(2,1)S(1)} %bitcast.35), channel_id=1, source_target_pairs={{0,12},{4,8},{8,4},{12,0},{1,13},{5,9},{9,5},{13,1},{2,14},{6,10},... | collective-permute-start | bytes 884744 | tf_op jit(solution)/shard_map/ppermute | solution.py:247
  119.8 4.5 %collective-permute-done.6 = bf16[1,384,384]{2,1,0:T(8,128)(2,1)S(1)} collective-permute-done((bf16[1,384,384]{2,1,0:T(8,128)(2,1)S(1)}, bf16[1,384,384]{2,1,0:T(8,128)(2,1)S(1)}, u32[]{:S(2)}, u32[]{:S(2)}) %collective-permute-start.6) | collective-permute-done | bytes 294944 | tf_op jit(solution)/shard_map/ppermute | solution.py:247
  124.4 3.6 collective-permute-done.5
  130.2 12.0 %all-gather.3.cloned.1.call-done.refs_1_ = bf16[256,3072]{1,0:T(8,128)(2,1)} async-done(((bf16[16,3072]{1,0:T(8,128)(2,1)}), bf16[256,3072]{1,0:T(8,128)(2,1)}) %all-gather.3.cloned.1.call-update) | async-done | bytes 1572880 | tf_op jit(solution)/shard_map/all_gather | solution.py:231
  146.8 4.6 %collective-permute-start.1 = (bf16[128,3072]{1,0:T(8,128)(2,1)}, bf16[128,3072]{1,0:T(8,128)(2,1)}, u32[]{:S(2)}, u32[]{:S(2)}) collective-permute-start(bf16[128,3072]{1,0:T(8,128)(2,1)} %get-tuple-element.9), channel_id=1, source_target_pairs={{0,6},{2,0},{4,2},{6,4},{1,7},{3,1},{5,3},{7,5},{8,14},{10,8},{12,... | collective-permute-start | bytes 2359304 | tf_op jit(solution)/shard_map/ppermute | solution.py:43
  151.4 9.0 %collective-permute-done.refs_2_ = bf16[128,3072]{1,0:T(8,128)(2,1)S(1)} collective-permute-done((bf16[128,3072]{1,0:T(8,128)(2,1)}, bf16[128,3072]{1,0:T(8,128)(2,1)S(1)}, u32[]{:S(2)}, u32[]{:S(2)}) %collective-permute-start) | collective-permute-done | bytes 786464 | tf_op jit(solution)/shard_map/ppermute | solution.py:43
  161.5 5.7 %project.1 = (bf16[512,128]{1,0:T(8,128)(2,1)}, bf16[512,256]{1,0:T(8,128)(2,1)}) custom-call(s32[1]{0:T(128)} %bitcast.1.refs_0_, bf16[256,3072]{1,0:T(8,128)(2,1)} %all-gather.3.cloned.1.call-done.refs_1_, bf16[128,3072]{1,0:T(8,128)(2,1)} %copy-done.7, bf16[128,3072]{1,0:T(8,128)(2,1)} %collective-permute-done.1.refs_3_, bf16[4,384,384]{2,1,0:T(8,128)(2,1)} %copy-done.2, ...), custom_call_target="tpu_custom_call" | custom-call | tf_op jit(solution)/shard_map/project/pallas_call | solution.py:92
  168.3 14.3 %all_to_all.25 = bf16[4,512,256]{2,1,0:T(8,128)(2,1)S(1)} all-to-all(bf16[4,512,256]{2,1,0:T(8,128)(2,1)S(1)} %broadcast_in_dim.27), channel_id=1, replica_groups=mesh['clip'=2,'big'=8,'zh'=2,'zn'=2,'xt'=2,'xu'=2,'head'=2] {'zn','xt'}, dimensions={0} | all-to-all | bytes 2097152 | tf_op jit(solution)/shard_map/all_to_all | solution.py:255
  182.5 10.4 %collective-permute-start.8 = (bf16[2048,256]{1,0:T(8,128)(2,1)S(1)}, bf16[2048,256]{1,0:T(8,128)(2,1)S(1)}, u32[]{:S(2)}, u32[]{:S(2)}) collective-permute-start(bf16[2048,256]{1,0:T(8,128)(2,1)S(1)} %bitcast.31), channel_id=1, source_target_pairs={{0,1},{1,0},{2,3},{3,2},{4,5},{5,4},{6,7},{7,6},{8,9},{9,8},{10,11... | collective-permute-start | bytes 3145736 | tf_op jit(solution)/shard_map/ppermute | solution.py:38
  196.1 4.2 %attend.3 = bf16[256,128]{1,0:T(8,128)(2,1)} custom-call(bf16[512,128]{1,0:T(8,128)(2,1)} %get-tuple-element.7.refs_0_, bf16[2048,256]{1,0:T(8,128)(2,1)} %bitcast.32, bf16[2048,256]{1,0:T(8,128)(2,1)} %copy-done.3), custom_call_target="tpu_custom_call" | custom-call | tf_op jit(solution)/shard_map/attend/pallas_call | solution.py:143
  201.1 4.0 %collective-permute-start.10 = (bf16[128,128]{1,0:T(8,128)(2,1)S(1)}, bf16[128,128]{1,0:T(8,128)(2,1)S(1)}, u32[]{:S(2)}, u32[]{:S(2)}) collective-permute-start(bf16[128,128]{1,0:T(8,128)(2,1)S(1)} %get-tuple-element.25), channel_id=1, source_target_pairs={{0,2},{2,4},{4,6},{6,0},{1,3},{3,5},{5,7},{7,1},{8,10},{10,12},{12... | collective-permute-start | bytes 98312 | tf_op jit(solution)/shard_map/ppermute | solution.py:43
  207.7 4.2 %attend.2 = bf16[256,128]{1,0:T(8,128)(2,1)} custom-call(bf16[512,128]{1,0:T(8,128)(2,1)} %get-tuple-element.7.refs_0_, bf16[2048,256]{1,0:T(8,128)(2,1)} %bitcast.33, bf16[2048,256]{1,0:T(8,128)(2,1)} %copy-done.3), custom_call_target="tpu_custom_call" | custom-call | tf_op jit(solution)/shard_map/attend/pallas_call | solution.py:143
  213.0 35.4 %all_to_all.26 = bf16[16,16,256]{2,1,0:T(8,128)(2,1)S(1)} all-to-all(bf16[16,16,256]{2,1,0:T(8,128)(2,1)S(1)} %maximum_select_fusion), channel_id=1, replica_groups=mesh['clip'=2,'big'=8,'zh'=2,'zn'=2,'xt'=2,'xu'=2,'head'=2] {'big','zh'}, dimensions={0} | all-to-all | bytes 262144 | tf_op jit(solution)/shard_map/all_to_all | solution.py:264
  249.6 3.8 all-to-all-start.3
  254.2 79.5 %all-gather.5.cloned.1.call-done = bf16[1536,384]{1,0:T(8,128)(2,1)} async-done(((bf16[96,384]{1,0:T(8,128)(2,1)}), bf16[1536,384]{1,0:T(8,128)(2,1)}) %all-gather.5.cloned.1.call-update) | async-done | bytes 1179664 | tf_op jit(solution)/shard_map/all_gather | solution.py:270
  335.1 4.3 %collective-permute-start.13 = (bf16[384,384]{1,0:T(8,128)(2,1)S(1)}, bf16[384,384]{1,0:T(8,128)(2,1)S(1)}, u32[]{:S(2)}, u32[]{:S(2)}) collective-permute-start(bf16[384,384]{1,0:T(8,128)(2,1)S(1)} %get-tuple-element.12), channel_id=1, source_target_pairs={{0,6},{2,0},{4,2},{6,4},{1,7},{3,1},{5,3},{7,5},{8,14},{10,8},{12,... | collective-permute-start | bytes 884744 | tf_op jit(solution)/shard_map/ppermute | solution.py:43
  345.1 3.4 collective-permute-done.12
  351.8 14.1 %collective-permute-start.14 = (bf16[4,384,384]{2,1,0:T(8,128)(2,1)S(1)}, bf16[4,384,384]{2,1,0:T(8,128)(2,1)S(1)}, u32[]{:S(2)}, u32[]{:S(2)}) collective-permute-start(bf16[4,384,384]{2,1,0:T(8,128)(2,1)S(1)} %pad_maximum_fusion.1.refs_2_), channel_id=1, source_target_pairs={{0,1},{1,0},{2,3},{3,2},{4,5},{5,4},{6,7},{7,6},{8,9},{9,8},{10,11... | collective-permute-start | bytes 3538952 | tf_op jit(solution)/shard_map/ppermute | solution.py:38
  369.6 3.4 combine.1
  373.0 8.8 %all_to_all.27 = bf16[8,16,384]{2,1,0:T(8,128)(2,1)S(1)} all-to-all(bf16[8,16,384]{2,1,0:T(8,128)(2,1)} %bitcast.43), channel_id=1, replica_groups=mesh['clip'=2,'big'=8,'zh'=2,'zn'=2,'xt'=2,'xu'=2,'head'=2] {'zn','xt','..., dimensions={0} | all-to-all | bytes 196608 | tf_op jit(solution)/shard_map/all_to_all | solution.py:282
  (69 shorter events, 43.3 us)
Async XLA Ops:
  6.5 135.6 %all-gather.3.cloned.1.call-start = ((), (), s32[]{:S(2)}) async-start(), calls=%async_computation.5 | async-start | bytes 1671168 | tf_op jit(solution)/shard_map/all_gather | solution.py:231
  10.8 0.7 collective-permute-start.2
  11.5 47.7 %collective-permute-start.3 = (bf16[3,96,384]{2,1,0:T(8,128)(2,1)S(1)}, bf16[3,96,384]{2,1,0:T(8,128)(2,1)S(1)}, u32[]{:S(2)}, u32[]{:S(2)}) collective-permute-start(bf16[3,96,384]{2,1,0:T(8,128)(2,1)S(1)} %collective-permute-done.2), channel_id=1, source_target_pairs={{0,0},{1,32},{2,66},{3,98},{4,132},{5,164},{6,198},{7,230},{10,2},... | collective-permute-start | bytes 663560 | tf_op jit(solution)/shard_map/ppermute | solution.py:199
  60.0 29.5 %all-to-all-start = ((bf16[4,96,384]{2,1,0:T(8,128)(2,1)}), bf16[4,96,384]{2,1,0:T(8,128)(2,1)S(1)}, u32[]{:S(2)}, u32[]{:S(2)}) async-start(bf16[4,96,384]{2,1,0:T(8,128)(2,1)} %concatenate.36), calls=%async_computation | async-start | bytes 589824 | tf_op jit(solution)/shard_map/all_to_all | solution.py:203
  89.5 34.9 %collective-permute-start.6 = (bf16[1,384,384]{2,1,0:T(8,128)(2,1)S(1)}, bf16[1,384,384]{2,1,0:T(8,128)(2,1)S(1)}, u32[]{:S(2)}, u32[]{:S(2)}) collective-permute-start(bf16[1,384,384]{2,1,0:T(8,128)(2,1)S(1)} %bitcast.35), channel_id=1, source_target_pairs={{0,12},{4,8},{8,4},{12,0},{1,13},{5,9},{9,5},{13,1},{2,14},{6,10},... | collective-permute-start | bytes 884744 | tf_op jit(solution)/shard_map/ppermute | solution.py:247
  115.6 12.4 %collective-permute-start.5 = (bf16[1,384,384]{2,1,0:T(8,128)(2,1)S(1)}, bf16[1,384,384]{2,1,0:T(8,128)(2,1)S(1)}, u32[]{:S(2)}, u32[]{:S(2)}) collective-permute-start(bf16[1,384,384]{2,1,0:T(8,128)(2,1)S(1)} %bitcast.36), channel_id=1, source_target_pairs={{0,8},{8,0},{1,9},{9,1},{2,10},{10,2},{3,11},{11,3},{4,12},{12,4},... | collective-permute-start | bytes 884744 | tf_op jit(solution)/shard_map/ppermute | solution.py:38
  117.6 10.4 %collective-permute-start.4 = (bf16[1,384,384]{2,1,0:T(8,128)(2,1)S(1)}, bf16[1,384,384]{2,1,0:T(8,128)(2,1)S(1)}, u32[]{:S(2)}, u32[]{:S(2)}) collective-permute-start(bf16[1,384,384]{2,1,0:T(8,128)(2,1)S(1)} %bitcast.37), channel_id=1, source_target_pairs={{0,4},{4,0},{1,5},{5,1},{2,6},{6,2},{3,7},{7,3},{8,12},{12,8},{9,1... | collective-permute-start | bytes 884744 | tf_op jit(solution)/shard_map/ppermute | solution.py:38
  128.2 16.7 %copy-start.2 = (bf16[4,384,384]{2,1,0:T(8,128)(2,1)}, bf16[4,384,384]{2,1,0:T(8,128)(2,1)S(1)}, u32[]{:S(2)}) copy-start(bf16[4,384,384]{2,1,0:T(8,128)(2,1)S(1)} %pad_maximum_fusion.refs_4_) | copy-start | bytes 3538948
  128.2 23.2 %collective-permute-start.7 = (bf16[4,384,384]{2,1,0:T(8,128)(2,1)S(1)}, bf16[4,384,384]{2,1,0:T(8,128)(2,1)S(1)}, u32[]{:S(2)}, u32[]{:S(2)}) collective-permute-start(bf16[4,384,384]{2,1,0:T(8,128)(2,1)S(1)} %pad_maximum_fusion.refs_4_), channel_id=1, source_target_pairs={{0,1},{1,0},{2,3},{3,2},{4,5},{5,4},{6,7},{7,6},{8,9},{9,8},{10,11... | collective-permute-start | bytes 3538952 | tf_op jit(solution)/shard_map/ppermute | solution.py:38
  144.8 15.6 %collective-permute-start = (bf16[128,3072]{1,0:T(8,128)(2,1)}, bf16[128,3072]{1,0:T(8,128)(2,1)S(1)}, u32[]{:S(2)}, u32[]{:S(2)}) collective-permute-start(bf16[128,3072]{1,0:T(8,128)(2,1)} %get-tuple-element.10), channel_id=1, source_target_pairs={{0,2},{2,4},{4,6},{6,0},{1,3},{3,5},{5,7},{7,1},{8,10},{10,12},{12... | collective-permute-start | bytes 2359304 | tf_op jit(solution)/shard_map/ppermute | solution.py:43
  146.8 14.7 %collective-permute-start.1 = (bf16[128,3072]{1,0:T(8,128)(2,1)}, bf16[128,3072]{1,0:T(8,128)(2,1)}, u32[]{:S(2)}, u32[]{:S(2)}) collective-permute-start(bf16[128,3072]{1,0:T(8,128)(2,1)} %get-tuple-element.9), channel_id=1, source_target_pairs={{0,6},{2,0},{4,2},{6,4},{1,7},{3,1},{5,3},{7,5},{8,14},{10,8},{12,... | collective-permute-start | bytes 2359304 | tf_op jit(solution)/shard_map/ppermute | solution.py:43
  151.4 10.1 %copy-start.6 = (bf16[4,384,384]{2,1,0:T(8,128)(2,1)}, bf16[4,384,384]{2,1,0:T(8,128)(2,1)S(1)}, u32[]{:S(2)}) copy-start(bf16[4,384,384]{2,1,0:T(8,128)(2,1)S(1)} %collective-permute-done.7.refs_5_) | copy-start | bytes 3538948
  182.5 12.6 %copy-start = (bf16[4,512,256]{2,1,0:T(8,128)(2,1)}, bf16[4,512,256]{2,1,0:T(8,128)(2,1)S(1)}, u32[]{:S(2)}) copy-start(bf16[4,512,256]{2,1,0:T(8,128)(2,1)S(1)} %all_to_all.25) | copy-start | bytes 3145732
  182.5 12.6 %collective-permute-start.8 = (bf16[2048,256]{1,0:T(8,128)(2,1)S(1)}, bf16[2048,256]{1,0:T(8,128)(2,1)S(1)}, u32[]{:S(2)}, u32[]{:S(2)}) collective-permute-start(bf16[2048,256]{1,0:T(8,128)(2,1)S(1)} %bitcast.31), channel_id=1, source_target_pairs={{0,1},{1,0},{2,3},{3,2},{4,5},{5,4},{6,7},{7,6},{8,9},{9,8},{10,11... | collective-permute-start | bytes 3145736 | tf_op jit(solution)/shard_map/ppermute | solution.py:38
  201.1 10.8 %collective-permute-start.10 = (bf16[128,128]{1,0:T(8,128)(2,1)S(1)}, bf16[128,128]{1,0:T(8,128)(2,1)S(1)}, u32[]{:S(2)}, u32[]{:S(2)}) collective-permute-start(bf16[128,128]{1,0:T(8,128)(2,1)S(1)} %get-tuple-element.25), channel_id=1, source_target_pairs={{0,2},{2,4},{4,6},{6,0},{1,3},{3,5},{5,7},{7,1},{8,10},{10,12},{12... | collective-permute-start | bytes 98312 | tf_op jit(solution)/shard_map/ppermute | solution.py:43
  205.1 6.8 %collective-permute-start.9 = (bf16[128,128]{1,0:T(8,128)(2,1)S(1)}, bf16[128,128]{1,0:T(8,128)(2,1)S(1)}, u32[]{:S(2)}, u32[]{:S(2)}) collective-permute-start(bf16[128,128]{1,0:T(8,128)(2,1)S(1)} %get-tuple-element.24), channel_id=1, source_target_pairs={{0,6},{2,0},{4,2},{6,4},{1,7},{3,1},{5,3},{7,5},{8,14},{10,8},{12,... | collective-permute-start | bytes 98312 | tf_op jit(solution)/shard_map/ppermute | solution.py:43
  249.6 118.7 %all-to-all-start.3 = ((bf16[8,16,3072]{2,1,0:T(8,128)(2,1)}), bf16[8,16,3072]{2,1,0:T(8,128)(2,1)S(1)}, u32[]{:S(2)}, u32[]{:S(2)}) async-start(bf16[8,16,3072]{2,1,0:T(8,128)(2,1)} %broadcast_in_dim.28), calls=%async_computation.3 | async-start | bytes 1572864 | tf_op jit(solution)/shard_map/all_to_all | solution.py:268
  253.4 80.4 %all-gather.5.cloned.1.call-start = ((), (), s32[]{:S(2)}) async-start(), calls=%async_computation.6 | async-start | bytes 1253376 | tf_op jit(solution)/shard_map/all_gather | solution.py:270
  335.1 10.0 %collective-permute-start.13 = (bf16[384,384]{1,0:T(8,128)(2,1)S(1)}, bf16[384,384]{1,0:T(8,128)(2,1)S(1)}, u32[]{:S(2)}, u32[]{:S(2)}) collective-permute-start(bf16[384,384]{1,0:T(8,128)(2,1)S(1)} %get-tuple-element.12), channel_id=1, source_target_pairs={{0,6},{2,0},{4,2},{6,4},{1,7},{3,1},{5,3},{7,5},{8,14},{10,8},{12,... | collective-permute-start | bytes 884744 | tf_op jit(solution)/shard_map/ppermute | solution.py:43
  339.4 9.1 %collective-permute-start.12 = (bf16[384,384]{1,0:T(8,128)(2,1)S(1)}, bf16[384,384]{1,0:T(8,128)(2,1)S(1)}, u32[]{:S(2)}, u32[]{:S(2)}) collective-permute-start(bf16[384,384]{1,0:T(8,128)(2,1)S(1)} %get-tuple-element.13), channel_id=1, source_target_pairs={{0,4},{2,6},{4,0},{6,2},{1,5},{3,7},{5,1},{7,3},{8,12},{10,14},{12... | collective-permute-start | bytes 884744 | tf_op jit(solution)/shard_map/ppermute | solution.py:43
  342.3 9.3 %collective-permute-start.11 = (bf16[384,384]{1,0:T(8,128)(2,1)S(1)}, bf16[384,384]{1,0:T(8,128)(2,1)S(1)}, u32[]{:S(2)}, u32[]{:S(2)}) collective-permute-start(bf16[384,384]{1,0:T(8,128)(2,1)S(1)} %get-tuple-element.14), channel_id=1, source_target_pairs={{0,2},{2,4},{4,6},{6,0},{1,3},{3,5},{5,7},{7,1},{8,10},{10,12},{12... | collective-permute-start | bytes 884744 | tf_op jit(solution)/shard_map/ppermute | solution.py:43
  351.6 14.8 %copy-start.8 = (f32[1,3072]{1,0:T(1,128)S(1)}, f32[1,3072]{1,0:T(1,128)}, u32[]{:S(2)}) copy-start(f32[1,3072]{1,0:T(1,128)} %param.13) | copy-start | bytes 36868
  351.7 16.6 %copy-start.1 = (bf16[4,384,384]{2,1,0:T(8,128)(2,1)}, bf16[4,384,384]{2,1,0:T(8,128)(2,1)S(1)}, u32[]{:S(2)}) copy-start(bf16[4,384,384]{2,1,0:T(8,128)(2,1)S(1)} %pad_maximum_fusion.1.refs_2_) | copy-start | bytes 3538948
  351.8 16.6 %collective-permute-start.14 = (bf16[4,384,384]{2,1,0:T(8,128)(2,1)S(1)}, bf16[4,384,384]{2,1,0:T(8,128)(2,1)S(1)}, u32[]{:S(2)}, u32[]{:S(2)}) collective-permute-start(bf16[4,384,384]{2,1,0:T(8,128)(2,1)S(1)} %pad_maximum_fusion.1.refs_2_), channel_id=1, source_target_pairs={{0,1},{1,0},{2,3},{3,2},{4,5},{5,4},{6,7},{7,6},{8,9},{9,8},{10,11... | collective-permute-start | bytes 3538952 | tf_op jit(solution)/shard_map/ppermute | solution.py:38
  (4 other events, 4.3 us)
Sparse Core Ops, SparseCore 0:
  9.4 132.6 all-gather.2
  256.3 77.4 all-gather.4

commit v4 on v3

--- a/solution.py
+++ b/solution.py
@@ -61,8 +61,13 @@
 
 def project_body(place_ref, *refs, parts, pieces, head_dim):
     toks, w_refs = refs[:parts], refs[parts : parts + pieces]
-    qg_ref, kg_ref, q_ref, kv_ref = refs[parts + pieces :]
-    depth = w_refs[0].shape[-2]
+    qg_ref, kg_ref, q_ref, kv_ref, whole_ref = refs[parts + pieces :]
+    depth, k = w_refs[0].shape[-2], 0
+    for w_ref in w_refs:
+        for s in range(w_ref.shape[0]):
+            start = pl.multiple_of((place_ref[0] ^ k) * depth, 128)
+            whole_ref[pl.ds(start, depth), :] = w_ref[s]
+            k += 1
 
     def norm(shaped, gain):
         mean_square = jnp.mean(jnp.square(shaped), axis=-1, keepdims=True)
@@ -70,14 +75,7 @@
 
     row = 0
     for tok in toks:
-        acc, k = None, 0
-        for w_ref in w_refs:
-            for s in range(w_ref.shape[0]):
-                start = pl.multiple_of((place_ref[0] ^ k) * depth, 128)
-                term = jnp.dot(
-                    tok[:, pl.ds(start, depth)], w_ref[s], preferred_element_type=jnp.float32
-                )
-                acc, k = term if acc is None else acc + term, k + 1
+        acc = jnp.dot(tok[...], whole_ref[...], preferred_element_type=jnp.float32)
         mine = slice(row, row + tok.shape[0])
         q_ref[mine, :] = norm(acc[:, :head_dim], qg_ref[...])
         kv_ref[mine, :head_dim] = norm(acc[:, head_dim : 2 * head_dim], kg_ref[...])
@@ -86,7 +84,7 @@
 
 
 def project(place, toks, weights, query_gain, key_gain, head_dim):
-    rows = sum(t.shape[0] for t in toks)
+    rows, width = sum(t.shape[0] for t in toks), toks[0].shape[1]
     vmem = pl.BlockSpec(memory_space=pltpu.VMEM)
     smem = pl.BlockSpec(memory_space=pltpu.SMEM)
     return pl.pallas_call(
@@ -98,24 +96,22 @@
             jax.ShapeDtypeStruct((rows, head_dim), jnp.bfloat16),
             jax.ShapeDtypeStruct((rows, 2 * head_dim), jnp.bfloat16),
         ),
+        scratch_shapes=[pltpu.VMEM((width, weights[0].shape[-1]), jnp.bfloat16)],
         name="project",
     )(place, *toks, *weights, query_gain[None], key_gain[None])
 
 
 def attend_body(q_ref, *refs, head_dim, chunk):
     *kv_refs, out_ref, score_ref = refs
-    root = math.sqrt(head_dim)
+    scale = math.log2(math.e) / math.sqrt(head_dim)
     q = q_ref[...]
     top, at_key, spots = None, 0, []
     for kv in kv_refs:
         step = min(chunk, kv.shape[0])
         for start in range(0, kv.shape[0], step):
             keys = kv[start : start + step, :head_dim]
-            s = (
-                lax.dot_general(
-                    q, keys, (((1,), (1,)), ((), ())), preferred_element_type=jnp.float32
-                )
-                / root
+            s = lax.dot_general(
+                q, keys, (((1,), (1,)), ((), ())), preferred_element_type=jnp.float32
             )
             score_ref[:, at_key : at_key + step] = s
             m = jnp.max(s, axis=-1, keepdims=True)
@@ -124,7 +120,7 @@
             at_key += step
     total, acc = None, None
     for kv, start, spot, step in spots:
-        w = jnp.exp(score_ref[:, spot : spot + step] - top)
+        w = jnp.exp2((score_ref[:, spot : spot + step] - top) * scale)
         part = jnp.sum(w, axis=-1, keepdims=True)
         term = jnp.dot(
             w.astype(jnp.bfloat16),

time: 391 us -> 391 us (level)
  no operation moved by 1% of the time
where the time goes in v4:
time: 391 us; the launch traced here: 389 us
  waiting for transfers between devices  158 us (40%)
  starting transfers between devices  124 us (32%)
  blocking collectives  58.5 us (15%)
  Pallas kernels  19 us (5%)
  local copies, waits for them, and re-layouts  14.6 us (4%)
  between operations  13.8 us (4%)
    all_gather x1, waiting for transfers between devices, per_device(): out_far = lax.all_gather(out_weight.T, FAR, axis=0, tiled=True)  79.5 us
    all_to_all x1, blocking collectives, per_device(): lax.all_to_all(pair.reshape(far, own, 2 * head_dim), FAR, 0, 0, tiled=True)  35.4 us
    ppermute x5, starting transfers between devices, swapped(): return lax.ppermute(value, axes, [(i, n - 1 - i) for i in range(n)])  30.6 us
    ppermute x1, starting transfers between devices, per_device(): near[3] = lax.ppermute(piece, ('zn', 'xt'), [(i, 3 - i) for i in range(4)])  26.2 us
    ppermute x1, waiting for transfers between devices, weights_to_tile(): moved = lax.ppermute(moved, GROUP, move)  24.1 us
    ppermute x1, starting transfers between devices, weights_to_tile(): moved = lax.ppermute(moved, GROUP, move)  23.6 us
    ppermute x7, starting transfers between devices, around(): return lax.ppermute(value, axes, [(i, (i + shift) % n) for i in range(n)])  23 us
    ppermute x7, waiting for transfers between devices, around(): return lax.ppermute(value, axes, [(i, (i + shift) % n) for i in range(n)])  16.5 us
  transfers between devices with their start and end apart: 19, of which 12 were waited for; matrix products, arithmetic and copies ran while one was open for 2% of the time, Pallas kernels for 1%

profile of v4, /device:TPU:33, one launch (start us, length us, event | category | flops | bytes accessed | tf_op | source)
XLA Modules:
  0.0 389.2 jit_solution(7285670161287214692)
XLA Ops:
  11.5 23.6 %collective-permute-start.3 = (bf16[3,96,384]{2,1,0:T(8,128)(2,1)S(1)}, bf16[3,96,384]{2,1,0:T(8,128)(2,1)S(1)}, u32[]{:S(2)}, u32[]{:S(2)}) collective-permute-start(bf16[3,96,384]{2,1,0:T(8,128)(2,1)S(1)} %collective-permute-done.2), channel_id=1, source_target_pairs={{0,0},{1,32},{2,66},{3,98},{4,132},{5,164},{6,198},{7,230},{10,2},... | collective-permute-start | bytes 663560 | tf_op jit(solution)/shard_map/ppermute | solution.py:195
  35.2 24.1 %collective-permute-done.3 = bf16[3,96,384]{2,1,0:T(8,128)(2,1)S(1)} collective-permute-done((bf16[3,96,384]{2,1,0:T(8,128)(2,1)S(1)}, bf16[3,96,384]{2,1,0:T(8,128)(2,1)S(1)}, u32[]{:S(2)}, u32[]{:S(2)}) %collective-permute-start.3) | collective-permute-done | bytes 221216 | tf_op jit(solution)/shard_map/ppermute | solution.py:195
  60.0 15.8 %all-to-all-start = ((bf16[4,96,384]{2,1,0:T(8,128)(2,1)}), bf16[4,96,384]{2,1,0:T(8,128)(2,1)S(1)}, u32[]{:S(2)}, u32[]{:S(2)}) async-start(bf16[4,96,384]{2,1,0:T(8,128)(2,1)} %concatenate.36), calls=%async_computation | async-start | bytes 589824 | tf_op jit(solution)/shard_map/all_to_all | solution.py:199
  75.8 13.7 %all-to-all-done = bf16[4,96,384]{2,1,0:T(8,128)(2,1)S(1)} async-done(((bf16[4,96,384]{2,1,0:T(8,128)(2,1)}), bf16[4,96,384]{2,1,0:T(8,128)(2,1)S(1)}, u32[]{:S(2)}, u32[]{:S(2)}) %all-to-all-start) | async-done | bytes 294944 | tf_op jit(solution)/shard_map/all_to_all | solution.py:199
  89.5 26.2 %collective-permute-start.6 = (bf16[1,384,384]{2,1,0:T(8,128)(2,1)S(1)}, bf16[1,384,384]{2,1,0:T(8,128)(2,1)S(1)}, u32[]{:S(2)}, u32[]{:S(2)}) collective-permute-start(bf16[1,384,384]{2,1,0:T(8,128)(2,1)S(1)} %bitcast.35), channel_id=1, source_target_pairs={{0,12},{4,8},{8,4},{12,0},{1,13},{5,9},{9,5},{13,1},{2,14},{6,10},... | collective-permute-start | bytes 884744 | tf_op jit(solution)/shard_map/ppermute | solution.py:243
  119.8 4.5 %collective-permute-done.6 = bf16[1,384,384]{2,1,0:T(8,128)(2,1)S(1)} collective-permute-done((bf16[1,384,384]{2,1,0:T(8,128)(2,1)S(1)}, bf16[1,384,384]{2,1,0:T(8,128)(2,1)S(1)}, u32[]{:S(2)}, u32[]{:S(2)}) %collective-permute-start.6) | collective-permute-done | bytes 294944 | tf_op jit(solution)/shard_map/ppermute | solution.py:243
  124.4 3.6 collective-permute-done.5
  130.2 12.0 %all-gather.3.cloned.1.call-done.refs_1_ = bf16[256,3072]{1,0:T(8,128)(2,1)} async-done(((bf16[16,3072]{1,0:T(8,128)(2,1)}), bf16[256,3072]{1,0:T(8,128)(2,1)}) %all-gather.3.cloned.1.call-update) | async-done | bytes 1572880 | tf_op jit(solution)/shard_map/all_gather | solution.py:227
  146.8 4.6 %collective-permute-start.1 = (bf16[128,3072]{1,0:T(8,128)(2,1)}, bf16[128,3072]{1,0:T(8,128)(2,1)}, u32[]{:S(2)}, u32[]{:S(2)}) collective-permute-start(bf16[128,3072]{1,0:T(8,128)(2,1)} %get-tuple-element.9), channel_id=1, source_target_pairs={{0,6},{2,0},{4,2},{6,4},{1,7},{3,1},{5,3},{7,5},{8,14},{10,8},{12,... | collective-permute-start | bytes 2359304 | tf_op jit(solution)/shard_map/ppermute | solution.py:43
  151.4 9.0 %collective-permute-done.refs_2_ = bf16[128,3072]{1,0:T(8,128)(2,1)S(1)} collective-permute-done((bf16[128,3072]{1,0:T(8,128)(2,1)}, bf16[128,3072]{1,0:T(8,128)(2,1)S(1)}, u32[]{:S(2)}, u32[]{:S(2)}) %collective-permute-start) | collective-permute-done | bytes 786464 | tf_op jit(solution)/shard_map/ppermute | solution.py:43
  161.5 5.5 %project.1 = (bf16[512,128]{1,0:T(8,128)(2,1)}, bf16[512,256]{1,0:T(8,128)(2,1)}) custom-call(s32[1]{0:T(128)} %bitcast.1.refs_0_, bf16[256,3072]{1,0:T(8,128)(2,1)} %all-gather.3.cloned.1.call-done.refs_1_, bf16[128,3072]{1,0:T(8,128)(2,1)} %copy-done.7, bf16[128,3072]{1,0:T(8,128)(2,1)} %collective-permute-done.1.refs_3_, bf16[4,384,384]{2,1,0:T(8,128)(2,1)} %copy-done.2, ...), custom_call_target="tpu_custom_call" | custom-call | tf_op jit(solution)/shard_map/project/pallas_call | solution.py:90
  168.0 14.3 %all_to_all.25 = bf16[4,512,256]{2,1,0:T(8,128)(2,1)S(1)} all-to-all(bf16[4,512,256]{2,1,0:T(8,128)(2,1)S(1)} %broadcast_in_dim.27), channel_id=1, replica_groups=mesh['clip'=2,'big'=8,'zh'=2,'zn'=2,'xt'=2,'xu'=2,'head'=2] {'zn','xt'}, dimensions={0} | all-to-all | bytes 2097152 | tf_op jit(solution)/shard_map/all_to_all | solution.py:251
  182.3 10.4 %collective-permute-start.8 = (bf16[2048,256]{1,0:T(8,128)(2,1)S(1)}, bf16[2048,256]{1,0:T(8,128)(2,1)S(1)}, u32[]{:S(2)}, u32[]{:S(2)}) collective-permute-start(bf16[2048,256]{1,0:T(8,128)(2,1)S(1)} %bitcast.31), channel_id=1, source_target_pairs={{0,1},{1,0},{2,3},{3,2},{4,5},{5,4},{6,7},{7,6},{8,9},{9,8},{10,11... | collective-permute-start | bytes 3145736 | tf_op jit(solution)/shard_map/ppermute | solution.py:38
  195.9 4.1 %attend.3 = bf16[256,128]{1,0:T(8,128)(2,1)} custom-call(bf16[512,128]{1,0:T(8,128)(2,1)} %get-tuple-element.7.refs_0_, bf16[2048,256]{1,0:T(8,128)(2,1)} %bitcast.32, bf16[2048,256]{1,0:T(8,128)(2,1)} %copy-done.3), custom_call_target="tpu_custom_call" | custom-call | tf_op jit(solution)/shard_map/attend/pallas_call | solution.py:139
  200.8 4.0 %collective-permute-start.10 = (bf16[128,128]{1,0:T(8,128)(2,1)S(1)}, bf16[128,128]{1,0:T(8,128)(2,1)S(1)}, u32[]{:S(2)}, u32[]{:S(2)}) collective-permute-start(bf16[128,128]{1,0:T(8,128)(2,1)S(1)} %get-tuple-element.25), channel_id=1, source_target_pairs={{0,2},{2,4},{4,6},{6,0},{1,3},{3,5},{5,7},{7,1},{8,10},{10,12},{12... | collective-permute-start | bytes 98312 | tf_op jit(solution)/shard_map/ppermute | solution.py:43
  207.4 4.1 %attend.2 = bf16[256,128]{1,0:T(8,128)(2,1)} custom-call(bf16[512,128]{1,0:T(8,128)(2,1)} %get-tuple-element.7.refs_0_, bf16[2048,256]{1,0:T(8,128)(2,1)} %bitcast.33, bf16[2048,256]{1,0:T(8,128)(2,1)} %copy-done.3), custom_call_target="tpu_custom_call" | custom-call | tf_op jit(solution)/shard_map/attend/pallas_call | solution.py:139
  212.5 35.4 %all_to_all.26 = bf16[16,16,256]{2,1,0:T(8,128)(2,1)S(1)} all-to-all(bf16[16,16,256]{2,1,0:T(8,128)(2,1)S(1)} %maximum_select_fusion), channel_id=1, replica_groups=mesh['clip'=2,'big'=8,'zh'=2,'zn'=2,'xt'=2,'xu'=2,'head'=2] {'big','zh'}, dimensions={0} | all-to-all | bytes 262144 | tf_op jit(solution)/shard_map/all_to_all | solution.py:260
  249.1 3.8 all-to-all-start.3
  253.8 79.5 %all-gather.5.cloned.1.call-done = bf16[1536,384]{1,0:T(8,128)(2,1)} async-done(((bf16[96,384]{1,0:T(8,128)(2,1)}), bf16[1536,384]{1,0:T(8,128)(2,1)}) %all-gather.5.cloned.1.call-update) | async-done | bytes 1179664 | tf_op jit(solution)/shard_map/all_gather | solution.py:266
  334.6 4.3 %collective-permute-start.13 = (bf16[384,384]{1,0:T(8,128)(2,1)S(1)}, bf16[384,384]{1,0:T(8,128)(2,1)S(1)}, u32[]{:S(2)}, u32[]{:S(2)}) collective-permute-start(bf16[384,384]{1,0:T(8,128)(2,1)S(1)} %get-tuple-element.12), channel_id=1, source_target_pairs={{0,6},{2,0},{4,2},{6,4},{1,7},{3,1},{5,3},{7,5},{8,14},{10,8},{12,... | collective-permute-start | bytes 884744 | tf_op jit(solution)/shard_map/ppermute | solution.py:43
  344.6 3.4 collective-permute-done.12
  351.3 14.1 %collective-permute-start.14 = (bf16[4,384,384]{2,1,0:T(8,128)(2,1)S(1)}, bf16[4,384,384]{2,1,0:T(8,128)(2,1)S(1)}, u32[]{:S(2)}, u32[]{:S(2)}) collective-permute-start(bf16[4,384,384]{2,1,0:T(8,128)(2,1)S(1)} %pad_maximum_fusion.1.refs_2_), channel_id=1, source_target_pairs={{0,1},{1,0},{2,3},{3,2},{4,5},{5,4},{6,7},{7,6},{8,9},{9,8},{10,11... | collective-permute-start | bytes 3538952 | tf_op jit(solution)/shard_map/ppermute | solution.py:38
  369.1 3.4 combine.1
  372.5 8.8 %all_to_all.27 = bf16[8,16,384]{2,1,0:T(8,128)(2,1)S(1)} all-to-all(bf16[8,16,384]{2,1,0:T(8,128)(2,1)} %bitcast.43), channel_id=1, replica_groups=mesh['clip'=2,'big'=8,'zh'=2,'zn'=2,'xt'=2,'xu'=2,'head'=2] {'zn','xt','..., dimensions={0} | all-to-all | bytes 196608 | tf_op jit(solution)/shard_map/all_to_all | solution.py:278
  (69 shorter events, 43.3 us)
Async XLA Ops:
  6.5 135.6 %all-gather.3.cloned.1.call-start = ((), (), s32[]{:S(2)}) async-start(), calls=%async_computation.5 | async-start | bytes 1671168 | tf_op jit(solution)/shard_map/all_gather | solution.py:227
  10.8 0.7 collective-permute-start.2
  11.5 47.7 %collective-permute-start.3 = (bf16[3,96,384]{2,1,0:T(8,128)(2,1)S(1)}, bf16[3,96,384]{2,1,0:T(8,128)(2,1)S(1)}, u32[]{:S(2)}, u32[]{:S(2)}) collective-permute-start(bf16[3,96,384]{2,1,0:T(8,128)(2,1)S(1)} %collective-permute-done.2), channel_id=1, source_target_pairs={{0,0},{1,32},{2,66},{3,98},{4,132},{5,164},{6,198},{7,230},{10,2},... | collective-permute-start | bytes 663560 | tf_op jit(solution)/shard_map/ppermute | solution.py:195
  60.0 29.5 %all-to-all-start = ((bf16[4,96,384]{2,1,0:T(8,128)(2,1)}), bf16[4,96,384]{2,1,0:T(8,128)(2,1)S(1)}, u32[]{:S(2)}, u32[]{:S(2)}) async-start(bf16[4,96,384]{2,1,0:T(8,128)(2,1)} %concatenate.36), calls=%async_computation | async-start | bytes 589824 | tf_op jit(solution)/shard_map/all_to_all | solution.py:199
  89.5 34.9 %collective-permute-start.6 = (bf16[1,384,384]{2,1,0:T(8,128)(2,1)S(1)}, bf16[1,384,384]{2,1,0:T(8,128)(2,1)S(1)}, u32[]{:S(2)}, u32[]{:S(2)}) collective-permute-start(bf16[1,384,384]{2,1,0:T(8,128)(2,1)S(1)} %bitcast.35), channel_id=1, source_target_pairs={{0,12},{4,8},{8,4},{12,0},{1,13},{5,9},{9,5},{13,1},{2,14},{6,10},... | collective-permute-start | bytes 884744 | tf_op jit(solution)/shard_map/ppermute | solution.py:243
  115.6 12.4 %collective-permute-start.5 = (bf16[1,384,384]{2,1,0:T(8,128)(2,1)S(1)}, bf16[1,384,384]{2,1,0:T(8,128)(2,1)S(1)}, u32[]{:S(2)}, u32[]{:S(2)}) collective-permute-start(bf16[1,384,384]{2,1,0:T(8,128)(2,1)S(1)} %bitcast.36), channel_id=1, source_target_pairs={{0,8},{8,0},{1,9},{9,1},{2,10},{10,2},{3,11},{11,3},{4,12},{12,4},... | collective-permute-start | bytes 884744 | tf_op jit(solution)/shard_map/ppermute | solution.py:38
  117.6 10.4 %collective-permute-start.4 = (bf16[1,384,384]{2,1,0:T(8,128)(2,1)S(1)}, bf16[1,384,384]{2,1,0:T(8,128)(2,1)S(1)}, u32[]{:S(2)}, u32[]{:S(2)}) collective-permute-start(bf16[1,384,384]{2,1,0:T(8,128)(2,1)S(1)} %bitcast.37), channel_id=1, source_target_pairs={{0,4},{4,0},{1,5},{5,1},{2,6},{6,2},{3,7},{7,3},{8,12},{12,8},{9,1... | collective-permute-start | bytes 884744 | tf_op jit(solution)/shard_map/ppermute | solution.py:38
  128.2 16.7 %copy-start.2 = (bf16[4,384,384]{2,1,0:T(8,128)(2,1)}, bf16[4,384,384]{2,1,0:T(8,128)(2,1)S(1)}, u32[]{:S(2)}) copy-start(bf16[4,384,384]{2,1,0:T(8,128)(2,1)S(1)} %pad_maximum_fusion.refs_4_) | copy-start | bytes 3538948
  128.2 23.2 %collective-permute-start.7 = (bf16[4,384,384]{2,1,0:T(8,128)(2,1)S(1)}, bf16[4,384,384]{2,1,0:T(8,128)(2,1)S(1)}, u32[]{:S(2)}, u32[]{:S(2)}) collective-permute-start(bf16[4,384,384]{2,1,0:T(8,128)(2,1)S(1)} %pad_maximum_fusion.refs_4_), channel_id=1, source_target_pairs={{0,1},{1,0},{2,3},{3,2},{4,5},{5,4},{6,7},{7,6},{8,9},{9,8},{10,11... | collective-permute-start | bytes 3538952 | tf_op jit(solution)/shard_map/ppermute | solution.py:38
  144.8 15.6 %collective-permute-start = (bf16[128,3072]{1,0:T(8,128)(2,1)}, bf16[128,3072]{1,0:T(8,128)(2,1)S(1)}, u32[]{:S(2)}, u32[]{:S(2)}) collective-permute-start(bf16[128,3072]{1,0:T(8,128)(2,1)} %get-tuple-element.10), channel_id=1, source_target_pairs={{0,2},{2,4},{4,6},{6,0},{1,3},{3,5},{5,7},{7,1},{8,10},{10,12},{12... | collective-permute-start | bytes 2359304 | tf_op jit(solution)/shard_map/ppermute | solution.py:43
  146.8 14.7 %collective-permute-start.1 = (bf16[128,3072]{1,0:T(8,128)(2,1)}, bf16[128,3072]{1,0:T(8,128)(2,1)}, u32[]{:S(2)}, u32[]{:S(2)}) collective-permute-start(bf16[128,3072]{1,0:T(8,128)(2,1)} %get-tuple-element.9), channel_id=1, source_target_pairs={{0,6},{2,0},{4,2},{6,4},{1,7},{3,1},{5,3},{7,5},{8,14},{10,8},{12,... | collective-permute-start | bytes 2359304 | tf_op jit(solution)/shard_map/ppermute | solution.py:43
  151.4 10.1 %copy-start.6 = (bf16[4,384,384]{2,1,0:T(8,128)(2,1)}, bf16[4,384,384]{2,1,0:T(8,128)(2,1)S(1)}, u32[]{:S(2)}) copy-start(bf16[4,384,384]{2,1,0:T(8,128)(2,1)S(1)} %collective-permute-done.7.refs_5_) | copy-start | bytes 3538948
  182.3 12.6 %copy-start = (bf16[4,512,256]{2,1,0:T(8,128)(2,1)}, bf16[4,512,256]{2,1,0:T(8,128)(2,1)S(1)}, u32[]{:S(2)}) copy-start(bf16[4,512,256]{2,1,0:T(8,128)(2,1)S(1)} %all_to_all.25) | copy-start | bytes 3145732
  182.3 12.6 %collective-permute-start.8 = (bf16[2048,256]{1,0:T(8,128)(2,1)S(1)}, bf16[2048,256]{1,0:T(8,128)(2,1)S(1)}, u32[]{:S(2)}, u32[]{:S(2)}) collective-permute-start(bf16[2048,256]{1,0:T(8,128)(2,1)S(1)} %bitcast.31), channel_id=1, source_target_pairs={{0,1},{1,0},{2,3},{3,2},{4,5},{5,4},{6,7},{7,6},{8,9},{9,8},{10,11... | collective-permute-start | bytes 3145736 | tf_op jit(solution)/shard_map/ppermute | solution.py:38
  200.8 10.7 %collective-permute-start.10 = (bf16[128,128]{1,0:T(8,128)(2,1)S(1)}, bf16[128,128]{1,0:T(8,128)(2,1)S(1)}, u32[]{:S(2)}, u32[]{:S(2)}) collective-permute-start(bf16[128,128]{1,0:T(8,128)(2,1)S(1)} %get-tuple-element.25), channel_id=1, source_target_pairs={{0,2},{2,4},{4,6},{6,0},{1,3},{3,5},{5,7},{7,1},{8,10},{10,12},{12... | collective-permute-start | bytes 98312 | tf_op jit(solution)/shard_map/ppermute | solution.py:43
  204.8 6.7 %collective-permute-start.9 = (bf16[128,128]{1,0:T(8,128)(2,1)S(1)}, bf16[128,128]{1,0:T(8,128)(2,1)S(1)}, u32[]{:S(2)}, u32[]{:S(2)}) collective-permute-start(bf16[128,128]{1,0:T(8,128)(2,1)S(1)} %get-tuple-element.24), channel_id=1, source_target_pairs={{0,6},{2,0},{4,2},{6,4},{1,7},{3,1},{5,3},{7,5},{8,14},{10,8},{12,... | collective-permute-start | bytes 98312 | tf_op jit(solution)/shard_map/ppermute | solution.py:43
  249.1 118.7 %all-to-all-start.3 = ((bf16[8,16,3072]{2,1,0:T(8,128)(2,1)}), bf16[8,16,3072]{2,1,0:T(8,128)(2,1)S(1)}, u32[]{:S(2)}, u32[]{:S(2)}) async-start(bf16[8,16,3072]{2,1,0:T(8,128)(2,1)} %broadcast_in_dim.28), calls=%async_computation.3 | async-start | bytes 1572864 | tf_op jit(solution)/shard_map/all_to_all | solution.py:264
  252.9 80.4 %all-gather.5.cloned.1.call-start = ((), (), s32[]{:S(2)}) async-start(), calls=%async_computation.6 | async-start | bytes 1253376 | tf_op jit(solution)/shard_map/all_gather | solution.py:266
  334.6 10.0 %collective-permute-start.13 = (bf16[384,384]{1,0:T(8,128)(2,1)S(1)}, bf16[384,384]{1,0:T(8,128)(2,1)S(1)}, u32[]{:S(2)}, u32[]{:S(2)}) collective-permute-start(bf16[384,384]{1,0:T(8,128)(2,1)S(1)} %get-tuple-element.12), channel_id=1, source_target_pairs={{0,6},{2,0},{4,2},{6,4},{1,7},{3,1},{5,3},{7,5},{8,14},{10,8},{12,... | collective-permute-start | bytes 884744 | tf_op jit(solution)/shard_map/ppermute | solution.py:43
  338.9 9.1 %collective-permute-start.12 = (bf16[384,384]{1,0:T(8,128)(2,1)S(1)}, bf16[384,384]{1,0:T(8,128)(2,1)S(1)}, u32[]{:S(2)}, u32[]{:S(2)}) collective-permute-start(bf16[384,384]{1,0:T(8,128)(2,1)S(1)} %get-tuple-element.13), channel_id=1, source_target_pairs={{0,4},{2,6},{4,0},{6,2},{1,5},{3,7},{5,1},{7,3},{8,12},{10,14},{12... | collective-permute-start | bytes 884744 | tf_op jit(solution)/shard_map/ppermute | solution.py:43
  341.8 9.3 %collective-permute-start.11 = (bf16[384,384]{1,0:T(8,128)(2,1)S(1)}, bf16[384,384]{1,0:T(8,128)(2,1)S(1)}, u32[]{:S(2)}, u32[]{:S(2)}) collective-permute-start(bf16[384,384]{1,0:T(8,128)(2,1)S(1)} %get-tuple-element.14), channel_id=1, source_target_pairs={{0,2},{2,4},{4,6},{6,0},{1,3},{3,5},{5,7},{7,1},{8,10},{10,12},{12... | collective-permute-start | bytes 884744 | tf_op jit(solution)/shard_map/ppermute | solution.py:43
  351.1 14.8 %copy-start.8 = (f32[1,3072]{1,0:T(1,128)S(1)}, f32[1,3072]{1,0:T(1,128)}, u32[]{:S(2)}) copy-start(f32[1,3072]{1,0:T(1,128)} %param.13) | copy-start | bytes 36868
  351.3 16.6 %copy-start.1 = (bf16[4,384,384]{2,1,0:T(8,128)(2,1)}, bf16[4,384,384]{2,1,0:T(8,128)(2,1)S(1)}, u32[]{:S(2)}) copy-start(bf16[4,384,384]{2,1,0:T(8,128)(2,1)S(1)} %pad_maximum_fusion.1.refs_2_) | copy-start | bytes 3538948
  351.3 16.6 %collective-permute-start.14 = (bf16[4,384,384]{2,1,0:T(8,128)(2,1)S(1)}, bf16[4,384,384]{2,1,0:T(8,128)(2,1)S(1)}, u32[]{:S(2)}, u32[]{:S(2)}) collective-permute-start(bf16[4,384,384]{2,1,0:T(8,128)(2,1)S(1)} %pad_maximum_fusion.1.refs_2_), channel_id=1, source_target_pairs={{0,1},{1,0},{2,3},{3,2},{4,5},{5,4},{6,7},{7,6},{8,9},{9,8},{10,11... | collective-permute-start | bytes 3538952 | tf_op jit(solution)/shard_map/ppermute | solution.py:38
  (4 other events, 4.3 us)
Sparse Core Ops, SparseCore 0:
  9.4 132.6 all-gather.2
  255.8 77.4 all-gather.4

commit v5 on v4

--- a/solution.py
+++ b/solution.py
@@ -9,7 +9,6 @@
 from jax.sharding import PartitionSpec as P
 
 EPSILON = 1e-06
-BIG = 8
 OUTER = ("big", "zh", "zn")
 INNER = ("xt", "xu")
 GROUP = (*OUTER, *INNER, "head")
@@ -78,12 +77,15 @@
         acc = jnp.dot(tok[...], whole_ref[...], preferred_element_type=jnp.float32)
         mine = slice(row, row + tok.shape[0])
         q_ref[mine, :] = norm(acc[:, :head_dim], qg_ref[...])
-        kv_ref[mine, :head_dim] = norm(acc[:, head_dim : 2 * head_dim], kg_ref[...])
-        kv_ref[mine, head_dim:] = acc[:, 2 * head_dim :].astype(jnp.bfloat16)
+        keys = norm(acc[:, head_dim : 2 * head_dim], kg_ref[...])
+        values = acc[:, 2 * head_dim :].astype(jnp.bfloat16)
+        for copy in range(kv_ref.shape[0]):
+            kv_ref[copy, mine, :head_dim] = keys
+            kv_ref[copy, mine, head_dim:] = values
         row += tok.shape[0]
 
 
-def project(place, toks, weights, query_gain, key_gain, head_dim):
+def project(place, toks, weights, query_gain, key_gain, head_dim, copies):
     rows, width = sum(t.shape[0] for t in toks), toks[0].shape[1]
     vmem = pl.BlockSpec(memory_space=pltpu.VMEM)
     smem = pl.BlockSpec(memory_space=pltpu.SMEM)
@@ -94,7 +96,7 @@
         in_specs=[smem] + [vmem] * (len(toks) + len(weights) + 2),
         out_shape=(
             jax.ShapeDtypeStruct((rows, head_dim), jnp.bfloat16),
-            jax.ShapeDtypeStruct((rows, 2 * head_dim), jnp.bfloat16),
+            jax.ShapeDtypeStruct((copies, rows, 2 * head_dim), jnp.bfloat16),
         ),
         scratch_shapes=[pltpu.VMEM((width, weights[0].shape[-1]), jnp.bfloat16)],
         name="project",
@@ -135,7 +137,7 @@
 def attend(query, kvs, head_dim, first, last):
     rows = 256
     keys = sum(kv.shape[0] for kv in kvs)
-    whole = [pl.BlockSpec(kv.shape, lambda i: (0, 0)) for kv in kvs]
+    whole = [pl.BlockSpec(memory_space=pltpu.VMEM)] * len(kvs)
     return pl.pallas_call(
         lambda *refs: attend_body(*refs, head_dim=head_dim, chunk=512),
         grid=((last - first) // rows,),
@@ -246,9 +248,11 @@
     odd_t = big // (2 * head)
     place = ((xt ^ odd_t) + 2 * zn + 4 * zc).astype(jnp.int32).reshape(1)
 
-    query, kv = project(place, [mine, left, right], weights, query_gain, key_gain, head_dim)
-    near = jnp.broadcast_to(kv, (lax.axis_size(("zn", "xt")), *kv.shape))
-    near = lax.all_to_all(near, ("zn", "xt"), 0, 0, tiled=True).reshape(-1, kv.shape[1])
+    copies = lax.axis_size(("zn", "xt"))
+    query, kv = project(
+        place, [mine, left, right], weights, query_gain, key_gain, head_dim, copies
+    )
+    near = lax.all_to_all(kv, ("zn", "xt"), 0, 0, tiled=True).reshape(-1, kv.shape[2])
     kvs = [near, swapped(near, "head")]
     away = attend(query, kvs, head_dim, 2 * half, 4 * half)
     theirs = [around(away[:half], INNER, -1), around(away[half:], INNER, 1)]
@@ -283,7 +287,8 @@
 def solution(mesh):
     shape = mesh.shape
     inner = shape["inner"]
-    split = (shape["clip"], BIG, 2, shape["outer"] // (2 * BIG), 2, inner // 2, shape["head"])
+    big = inner * shape["head"]
+    split = (shape["clip"], big, 2, shape["outer"] // (2 * big), 2, inner // 2, shape["head"])
     fine = Mesh(mesh.devices.reshape(split), ("clip", *GROUP))
     row = (*INNER, "head")
     in_specs = (

time: 391 us -> 390 us (level)
  no operation moved by 1% of the time
where the time goes in v5:
time: 390 us; the launch traced here: 389 us
  waiting for transfers between devices  158 us (41%)
  starting transfers between devices  124 us (32%)
  blocking collectives  58.6 us (15%)
  Pallas kernels  19.2 us (5%)
  between operations  13.8 us (4%)
  local copies, waits for them, and re-layouts  13.5 us (3%)
    all_gather x1, waiting for transfers between devices, per_device(): out_far = lax.all_gather(out_weight.T, FAR, axis=0, tiled=True)  79.5 us
    all_to_all x1, blocking collectives, per_device(): lax.all_to_all(pair.reshape(far, own, 2 * head_dim), FAR, 0, 0, tiled=True)  35.4 us
    ppermute x5, starting transfers between devices, swapped(): return lax.ppermute(value, axes, [(i, n - 1 - i) for i in range(n)])  30.6 us
    ppermute x1, starting transfers between devices, per_device(): near[3] = lax.ppermute(piece, ('zn', 'xt'), [(i, 3 - i) for i in range(4)])  26.2 us
    ppermute x1, waiting for transfers between devices, weights_to_tile(): moved = lax.ppermute(moved, GROUP, move)  24.1 us
    ppermute x1, starting transfers between devices, weights_to_tile(): moved = lax.ppermute(moved, GROUP, move)  23.6 us
    ppermute x7, starting transfers between devices, around(): return lax.ppermute(value, axes, [(i, (i + shift) % n) for i in range(n)])  23 us
    ppermute x7, waiting for transfers between devices, around(): return lax.ppermute(value, axes, [(i, (i + shift) % n) for i in range(n)])  16.5 us
  transfers between devices with their start and end apart: 19, of which 12 were waited for; matrix products, arithmetic and copies ran while one was open for 2% of the time, Pallas kernels for 1%

profile of v5, /device:TPU:33, one launch (start us, length us, event | category | flops | bytes accessed | tf_op | source)
XLA Modules:
  0.0 388.6 jit_solution(629754192363873509)
XLA Ops:
  11.5 23.6 %collective-permute-start.3 = (bf16[3,96,384]{2,1,0:T(8,128)(2,1)S(1)}, bf16[3,96,384]{2,1,0:T(8,128)(2,1)S(1)}, u32[]{:S(2)}, u32[]{:S(2)}) collective-permute-start(bf16[3,96,384]{2,1,0:T(8,128)(2,1)S(1)} %collective-permute-done.2), channel_id=1, source_target_pairs={{0,0},{1,32},{2,66},{3,98},{4,132},{5,164},{6,198},{7,230},{10,2},... | collective-permute-start | bytes 663560 | tf_op jit(solution)/shard_map/ppermute | solution.py:197
  35.2 24.1 %collective-permute-done.3 = bf16[3,96,384]{2,1,0:T(8,128)(2,1)S(1)} collective-permute-done((bf16[3,96,384]{2,1,0:T(8,128)(2,1)S(1)}, bf16[3,96,384]{2,1,0:T(8,128)(2,1)S(1)}, u32[]{:S(2)}, u32[]{:S(2)}) %collective-permute-start.3) | collective-permute-done | bytes 221216 | tf_op jit(solution)/shard_map/ppermute | solution.py:197
  60.0 15.8 %all-to-all-start = ((bf16[4,96,384]{2,1,0:T(8,128)(2,1)}), bf16[4,96,384]{2,1,0:T(8,128)(2,1)S(1)}, u32[]{:S(2)}, u32[]{:S(2)}) async-start(bf16[4,96,384]{2,1,0:T(8,128)(2,1)} %concatenate.36), calls=%async_computation | async-start | bytes 589824 | tf_op jit(solution)/shard_map/all_to_all | solution.py:201
  75.8 13.7 %all-to-all-done = bf16[4,96,384]{2,1,0:T(8,128)(2,1)S(1)} async-done(((bf16[4,96,384]{2,1,0:T(8,128)(2,1)}), bf16[4,96,384]{2,1,0:T(8,128)(2,1)S(1)}, u32[]{:S(2)}, u32[]{:S(2)}) %all-to-all-start) | async-done | bytes 294944 | tf_op jit(solution)/shard_map/all_to_all | solution.py:201
  89.5 26.2 %collective-permute-start.6 = (bf16[1,384,384]{2,1,0:T(8,128)(2,1)S(1)}, bf16[1,384,384]{2,1,0:T(8,128)(2,1)S(1)}, u32[]{:S(2)}, u32[]{:S(2)}) collective-permute-start(bf16[1,384,384]{2,1,0:T(8,128)(2,1)S(1)} %bitcast.35), channel_id=1, source_target_pairs={{0,12},{4,8},{8,4},{12,0},{1,13},{5,9},{9,5},{13,1},{2,14},{6,10},... | collective-permute-start | bytes 884744 | tf_op jit(solution)/shard_map/ppermute | solution.py:245
  119.8 4.5 %collective-permute-done.6 = bf16[1,384,384]{2,1,0:T(8,128)(2,1)S(1)} collective-permute-done((bf16[1,384,384]{2,1,0:T(8,128)(2,1)S(1)}, bf16[1,384,384]{2,1,0:T(8,128)(2,1)S(1)}, u32[]{:S(2)}, u32[]{:S(2)}) %collective-permute-start.6) | collective-permute-done | bytes 294944 | tf_op jit(solution)/shard_map/ppermute | solution.py:245
  124.4 3.6 collective-permute-done.5
  130.2 12.0 %all-gather.3.cloned.1.call-done.refs_1_ = bf16[256,3072]{1,0:T(8,128)(2,1)} async-done(((bf16[16,3072]{1,0:T(8,128)(2,1)}), bf16[256,3072]{1,0:T(8,128)(2,1)}) %all-gather.3.cloned.1.call-update) | async-done | bytes 1572880 | tf_op jit(solution)/shard_map/all_gather | solution.py:229
  146.7 4.6 %collective-permute-start.1 = (bf16[128,3072]{1,0:T(8,128)(2,1)}, bf16[128,3072]{1,0:T(8,128)(2,1)}, u32[]{:S(2)}, u32[]{:S(2)}) collective-permute-start(bf16[128,3072]{1,0:T(8,128)(2,1)} %get-tuple-element.9), channel_id=1, source_target_pairs={{0,6},{2,0},{4,2},{6,4},{1,7},{3,1},{5,3},{7,5},{8,14},{10,8},{12,... | collective-permute-start | bytes 2359304 | tf_op jit(solution)/shard_map/ppermute | solution.py:42
  151.4 9.0 %collective-permute-done.refs_2_ = bf16[128,3072]{1,0:T(8,128)(2,1)S(1)} collective-permute-done((bf16[128,3072]{1,0:T(8,128)(2,1)}, bf16[128,3072]{1,0:T(8,128)(2,1)S(1)}, u32[]{:S(2)}, u32[]{:S(2)}) %collective-permute-start) | collective-permute-done | bytes 786464 | tf_op jit(solution)/shard_map/ppermute | solution.py:42
  161.4 5.8 %project.1 = (bf16[512,128]{1,0:T(8,128)(2,1)}, bf16[4,512,256]{2,1,0:T(8,128)(2,1)}) custom-call(s32[1]{0:T(128)} %bitcast.1.refs_0_, bf16[256,3072]{1,0:T(8,128)(2,1)} %all-gather.3.cloned.1.call-done.refs_1_, bf16[128,3072]{1,0:T(8,128)(2,1)} %copy-done.7, bf16[128,3072]{1,0:T(8,128)(2,1)} %collective-permute-done.1.refs_3_, ...), custom_call_target="tpu_custom_call" | custom-call | tf_op jit(solution)/shard_map/project/pallas_call | solution.py:92
  167.2 14.5 %all_to_all.25 = bf16[4,512,256]{2,1,0:T(8,128)(2,1)S(1)} all-to-all(bf16[4,512,256]{2,1,0:T(8,128)(2,1)} %get-tuple-element.8), channel_id=1, replica_groups=mesh['clip'=2,'big'=8,'zh'=2,'zn'=2,'xt'=2,'xu'=2,'head'=2] {'zn','xt'}, dimensions={0} | all-to-all | bytes 2097152 | tf_op jit(solution)/shard_map/all_to_all | solution.py:255
  181.7 10.4 %collective-permute-start.8 = (bf16[2048,256]{1,0:T(8,128)(2,1)S(1)}, bf16[2048,256]{1,0:T(8,128)(2,1)S(1)}, u32[]{:S(2)}, u32[]{:S(2)}) collective-permute-start(bf16[2048,256]{1,0:T(8,128)(2,1)S(1)} %bitcast.31), channel_id=1, source_target_pairs={{0,1},{1,0},{2,3},{3,2},{4,5},{5,4},{6,7},{7,6},{8,9},{9,8},{10,11... | collective-permute-start | bytes 3145736 | tf_op jit(solution)/shard_map/ppermute | solution.py:37
  195.3 4.1 %attend.3 = bf16[256,128]{1,0:T(8,128)(2,1)} custom-call(bf16[512,128]{1,0:T(8,128)(2,1)} %get-tuple-element.7.refs_0_, bf16[2048,256]{1,0:T(8,128)(2,1)} %bitcast.32, bf16[2048,256]{1,0:T(8,128)(2,1)} %copy-done.3), custom_call_target="tpu_custom_call" | custom-call | tf_op jit(solution)/shard_map/attend/pallas_call | solution.py:141
  200.2 4.0 %collective-permute-start.10 = (bf16[128,128]{1,0:T(8,128)(2,1)S(1)}, bf16[128,128]{1,0:T(8,128)(2,1)S(1)}, u32[]{:S(2)}, u32[]{:S(2)}) collective-permute-start(bf16[128,128]{1,0:T(8,128)(2,1)S(1)} %get-tuple-element.25), channel_id=1, source_target_pairs={{0,2},{2,4},{4,6},{6,0},{1,3},{3,5},{5,7},{7,1},{8,10},{10,12},{12... | collective-permute-start | bytes 98312 | tf_op jit(solution)/shard_map/ppermute | solution.py:42
  206.8 4.1 %attend.2 = bf16[256,128]{1,0:T(8,128)(2,1)} custom-call(bf16[512,128]{1,0:T(8,128)(2,1)} %get-tuple-element.7.refs_0_, bf16[2048,256]{1,0:T(8,128)(2,1)} %bitcast.33, bf16[2048,256]{1,0:T(8,128)(2,1)} %copy-done.3), custom_call_target="tpu_custom_call" | custom-call | tf_op jit(solution)/shard_map/attend/pallas_call | solution.py:141
  211.9 35.4 %all_to_all.26 = bf16[16,16,256]{2,1,0:T(8,128)(2,1)S(1)} all-to-all(bf16[16,16,256]{2,1,0:T(8,128)(2,1)S(1)} %maximum_select_fusion), channel_id=1, replica_groups=mesh['clip'=2,'big'=8,'zh'=2,'zn'=2,'xt'=2,'xu'=2,'head'=2] {'big','zh'}, dimensions={0} | all-to-all | bytes 262144 | tf_op jit(solution)/shard_map/all_to_all | solution.py:264
  248.5 3.8 all-to-all-start.3
  253.2 79.5 %all-gather.5.cloned.1.call-done = bf16[1536,384]{1,0:T(8,128)(2,1)} async-done(((bf16[96,384]{1,0:T(8,128)(2,1)}), bf16[1536,384]{1,0:T(8,128)(2,1)}) %all-gather.5.cloned.1.call-update) | async-done | bytes 1179664 | tf_op jit(solution)/shard_map/all_gather | solution.py:270
  334.0 4.3 %collective-permute-start.13 = (bf16[384,384]{1,0:T(8,128)(2,1)S(1)}, bf16[384,384]{1,0:T(8,128)(2,1)S(1)}, u32[]{:S(2)}, u32[]{:S(2)}) collective-permute-start(bf16[384,384]{1,0:T(8,128)(2,1)S(1)} %get-tuple-element.12), channel_id=1, source_target_pairs={{0,6},{2,0},{4,2},{6,4},{1,7},{3,1},{5,3},{7,5},{8,14},{10,8},{12,... | collective-permute-start | bytes 884744 | tf_op jit(solution)/shard_map/ppermute | solution.py:42
  344.0 3.4 collective-permute-done.12
  350.7 14.1 %collective-permute-start.14 = (bf16[4,384,384]{2,1,0:T(8,128)(2,1)S(1)}, bf16[4,384,384]{2,1,0:T(8,128)(2,1)S(1)}, u32[]{:S(2)}, u32[]{:S(2)}) collective-permute-start(bf16[4,384,384]{2,1,0:T(8,128)(2,1)S(1)} %pad_maximum_fusion.1.refs_2_), channel_id=1, source_target_pairs={{0,1},{1,0},{2,3},{3,2},{4,5},{5,4},{6,7},{7,6},{8,9},{9,8},{10,11... | collective-permute-start | bytes 3538952 | tf_op jit(solution)/shard_map/ppermute | solution.py:37
  368.5 3.4 combine.1
  371.9 8.8 %all_to_all.27 = bf16[8,16,384]{2,1,0:T(8,128)(2,1)S(1)} all-to-all(bf16[8,16,384]{2,1,0:T(8,128)(2,1)} %bitcast.43), channel_id=1, replica_groups=mesh['clip'=2,'big'=8,'zh'=2,'zn'=2,'xt'=2,'xu'=2,'head'=2] {'zn','xt','..., dimensions={0} | all-to-all | bytes 196608 | tf_op jit(solution)/shard_map/all_to_all | solution.py:282
  (68 shorter events, 42.3 us)
Async XLA Ops:
  6.5 135.6 %all-gather.3.cloned.1.call-start = ((), (), s32[]{:S(2)}) async-start(), calls=%async_computation.5 | async-start | bytes 1671168 | tf_op jit(solution)/shard_map/all_gather | solution.py:229
  10.8 0.7 collective-permute-start.2
  11.5 47.7 %collective-permute-start.3 = (bf16[3,96,384]{2,1,0:T(8,128)(2,1)S(1)}, bf16[3,96,384]{2,1,0:T(8,128)(2,1)S(1)}, u32[]{:S(2)}, u32[]{:S(2)}) collective-permute-start(bf16[3,96,384]{2,1,0:T(8,128)(2,1)S(1)} %collective-permute-done.2), channel_id=1, source_target_pairs={{0,0},{1,32},{2,66},{3,98},{4,132},{5,164},{6,198},{7,230},{10,2},... | collective-permute-start | bytes 663560 | tf_op jit(solution)/shard_map/ppermute | solution.py:197
  60.0 29.5 %all-to-all-start = ((bf16[4,96,384]{2,1,0:T(8,128)(2,1)}), bf16[4,96,384]{2,1,0:T(8,128)(2,1)S(1)}, u32[]{:S(2)}, u32[]{:S(2)}) async-start(bf16[4,96,384]{2,1,0:T(8,128)(2,1)} %concatenate.36), calls=%async_computation | async-start | bytes 589824 | tf_op jit(solution)/shard_map/all_to_all | solution.py:201
  89.5 34.9 %collective-permute-start.6 = (bf16[1,384,384]{2,1,0:T(8,128)(2,1)S(1)}, bf16[1,384,384]{2,1,0:T(8,128)(2,1)S(1)}, u32[]{:S(2)}, u32[]{:S(2)}) collective-permute-start(bf16[1,384,384]{2,1,0:T(8,128)(2,1)S(1)} %bitcast.35), channel_id=1, source_target_pairs={{0,12},{4,8},{8,4},{12,0},{1,13},{5,9},{9,5},{13,1},{2,14},{6,10},... | collective-permute-start | bytes 884744 | tf_op jit(solution)/shard_map/ppermute | solution.py:245
  115.6 12.4 %collective-permute-start.5 = (bf16[1,384,384]{2,1,0:T(8,128)(2,1)S(1)}, bf16[1,384,384]{2,1,0:T(8,128)(2,1)S(1)}, u32[]{:S(2)}, u32[]{:S(2)}) collective-permute-start(bf16[1,384,384]{2,1,0:T(8,128)(2,1)S(1)} %bitcast.36), channel_id=1, source_target_pairs={{0,8},{8,0},{1,9},{9,1},{2,10},{10,2},{3,11},{11,3},{4,12},{12,4},... | collective-permute-start | bytes 884744 | tf_op jit(solution)/shard_map/ppermute | solution.py:37
  117.6 10.4 %collective-permute-start.4 = (bf16[1,384,384]{2,1,0:T(8,128)(2,1)S(1)}, bf16[1,384,384]{2,1,0:T(8,128)(2,1)S(1)}, u32[]{:S(2)}, u32[]{:S(2)}) collective-permute-start(bf16[1,384,384]{2,1,0:T(8,128)(2,1)S(1)} %bitcast.37), channel_id=1, source_target_pairs={{0,4},{4,0},{1,5},{5,1},{2,6},{6,2},{3,7},{7,3},{8,12},{12,8},{9,1... | collective-permute-start | bytes 884744 | tf_op jit(solution)/shard_map/ppermute | solution.py:37
  128.2 16.6 %copy-start.2 = (bf16[4,384,384]{2,1,0:T(8,128)(2,1)}, bf16[4,384,384]{2,1,0:T(8,128)(2,1)S(1)}, u32[]{:S(2)}) copy-start(bf16[4,384,384]{2,1,0:T(8,128)(2,1)S(1)} %pad_maximum_fusion.refs_4_) | copy-start | bytes 3538948
  128.2 23.2 %collective-permute-start.7 = (bf16[4,384,384]{2,1,0:T(8,128)(2,1)S(1)}, bf16[4,384,384]{2,1,0:T(8,128)(2,1)S(1)}, u32[]{:S(2)}, u32[]{:S(2)}) collective-permute-start(bf16[4,384,384]{2,1,0:T(8,128)(2,1)S(1)} %pad_maximum_fusion.refs_4_), channel_id=1, source_target_pairs={{0,1},{1,0},{2,3},{3,2},{4,5},{5,4},{6,7},{7,6},{8,9},{9,8},{10,11... | collective-permute-start | bytes 3538952 | tf_op jit(solution)/shard_map/ppermute | solution.py:37
  144.8 15.6 %collective-permute-start = (bf16[128,3072]{1,0:T(8,128)(2,1)}, bf16[128,3072]{1,0:T(8,128)(2,1)S(1)}, u32[]{:S(2)}, u32[]{:S(2)}) collective-permute-start(bf16[128,3072]{1,0:T(8,128)(2,1)} %get-tuple-element.10), channel_id=1, source_target_pairs={{0,2},{2,4},{4,6},{6,0},{1,3},{3,5},{5,7},{7,1},{8,10},{10,12},{12... | collective-permute-start | bytes 2359304 | tf_op jit(solution)/shard_map/ppermute | solution.py:42
  146.7 14.7 %collective-permute-start.1 = (bf16[128,3072]{1,0:T(8,128)(2,1)}, bf16[128,3072]{1,0:T(8,128)(2,1)}, u32[]{:S(2)}, u32[]{:S(2)}) collective-permute-start(bf16[128,3072]{1,0:T(8,128)(2,1)} %get-tuple-element.9), channel_id=1, source_target_pairs={{0,6},{2,0},{4,2},{6,4},{1,7},{3,1},{5,3},{7,5},{8,14},{10,8},{12,... | collective-permute-start | bytes 2359304 | tf_op jit(solution)/shard_map/ppermute | solution.py:42
  151.4 10.1 %copy-start.6 = (bf16[4,384,384]{2,1,0:T(8,128)(2,1)}, bf16[4,384,384]{2,1,0:T(8,128)(2,1)S(1)}, u32[]{:S(2)}) copy-start(bf16[4,384,384]{2,1,0:T(8,128)(2,1)S(1)} %collective-permute-done.7.refs_5_) | copy-start | bytes 3538948
  181.7 12.7 %copy-start = (bf16[4,512,256]{2,1,0:T(8,128)(2,1)}, bf16[4,512,256]{2,1,0:T(8,128)(2,1)S(1)}, u32[]{:S(2)}) copy-start(bf16[4,512,256]{2,1,0:T(8,128)(2,1)S(1)} %all_to_all.25) | copy-start | bytes 3145732
  181.7 12.7 %collective-permute-start.8 = (bf16[2048,256]{1,0:T(8,128)(2,1)S(1)}, bf16[2048,256]{1,0:T(8,128)(2,1)S(1)}, u32[]{:S(2)}, u32[]{:S(2)}) collective-permute-start(bf16[2048,256]{1,0:T(8,128)(2,1)S(1)} %bitcast.31), channel_id=1, source_target_pairs={{0,1},{1,0},{2,3},{3,2},{4,5},{5,4},{6,7},{7,6},{8,9},{9,8},{10,11... | collective-permute-start | bytes 3145736 | tf_op jit(solution)/shard_map/ppermute | solution.py:37
  200.2 10.7 %collective-permute-start.10 = (bf16[128,128]{1,0:T(8,128)(2,1)S(1)}, bf16[128,128]{1,0:T(8,128)(2,1)S(1)}, u32[]{:S(2)}, u32[]{:S(2)}) collective-permute-start(bf16[128,128]{1,0:T(8,128)(2,1)S(1)} %get-tuple-element.25), channel_id=1, source_target_pairs={{0,2},{2,4},{4,6},{6,0},{1,3},{3,5},{5,7},{7,1},{8,10},{10,12},{12... | collective-permute-start | bytes 98312 | tf_op jit(solution)/shard_map/ppermute | solution.py:42
  204.2 6.7 %collective-permute-start.9 = (bf16[128,128]{1,0:T(8,128)(2,1)S(1)}, bf16[128,128]{1,0:T(8,128)(2,1)S(1)}, u32[]{:S(2)}, u32[]{:S(2)}) collective-permute-start(bf16[128,128]{1,0:T(8,128)(2,1)S(1)} %get-tuple-element.24), channel_id=1, source_target_pairs={{0,6},{2,0},{4,2},{6,4},{1,7},{3,1},{5,3},{7,5},{8,14},{10,8},{12,... | collective-permute-start | bytes 98312 | tf_op jit(solution)/shard_map/ppermute | solution.py:42
  248.5 118.7 %all-to-all-start.3 = ((bf16[8,16,3072]{2,1,0:T(8,128)(2,1)}), bf16[8,16,3072]{2,1,0:T(8,128)(2,1)S(1)}, u32[]{:S(2)}, u32[]{:S(2)}) async-start(bf16[8,16,3072]{2,1,0:T(8,128)(2,1)} %broadcast_in_dim.24), calls=%async_computation.3 | async-start | bytes 1572864 | tf_op jit(solution)/shard_map/all_to_all | solution.py:268
  252.3 80.4 %all-gather.5.cloned.1.call-start = ((), (), s32[]{:S(2)}) async-start(), calls=%async_computation.6 | async-start | bytes 1253376 | tf_op jit(solution)/shard_map/all_gather | solution.py:270
  334.0 10.0 %collective-permute-start.13 = (bf16[384,384]{1,0:T(8,128)(2,1)S(1)}, bf16[384,384]{1,0:T(8,128)(2,1)S(1)}, u32[]{:S(2)}, u32[]{:S(2)}) collective-permute-start(bf16[384,384]{1,0:T(8,128)(2,1)S(1)} %get-tuple-element.12), channel_id=1, source_target_pairs={{0,6},{2,0},{4,2},{6,4},{1,7},{3,1},{5,3},{7,5},{8,14},{10,8},{12,... | collective-permute-start | bytes 884744 | tf_op jit(solution)/shard_map/ppermute | solution.py:42
  338.3 9.1 %collective-permute-start.12 = (bf16[384,384]{1,0:T(8,128)(2,1)S(1)}, bf16[384,384]{1,0:T(8,128)(2,1)S(1)}, u32[]{:S(2)}, u32[]{:S(2)}) collective-permute-start(bf16[384,384]{1,0:T(8,128)(2,1)S(1)} %get-tuple-element.13), channel_id=1, source_target_pairs={{0,4},{2,6},{4,0},{6,2},{1,5},{3,7},{5,1},{7,3},{8,12},{10,14},{12... | collective-permute-start | bytes 884744 | tf_op jit(solution)/shard_map/ppermute | solution.py:42
  341.2 9.3 %collective-permute-start.11 = (bf16[384,384]{1,0:T(8,128)(2,1)S(1)}, bf16[384,384]{1,0:T(8,128)(2,1)S(1)}, u32[]{:S(2)}, u32[]{:S(2)}) collective-permute-start(bf16[384,384]{1,0:T(8,128)(2,1)S(1)} %get-tuple-element.14), channel_id=1, source_target_pairs={{0,2},{2,4},{4,6},{6,0},{1,3},{3,5},{5,7},{7,1},{8,10},{10,12},{12... | collective-permute-start | bytes 884744 | tf_op jit(solution)/shard_map/ppermute | solution.py:42
  350.5 14.8 %copy-start.8 = (f32[1,3072]{1,0:T(1,128)S(1)}, f32[1,3072]{1,0:T(1,128)}, u32[]{:S(2)}) copy-start(f32[1,3072]{1,0:T(1,128)} %param.13) | copy-start | bytes 36868
  350.7 16.6 %copy-start.1 = (bf16[4,384,384]{2,1,0:T(8,128)(2,1)}, bf16[4,384,384]{2,1,0:T(8,128)(2,1)S(1)}, u32[]{:S(2)}) copy-start(bf16[4,384,384]{2,1,0:T(8,128)(2,1)S(1)} %pad_maximum_fusion.1.refs_2_) | copy-start | bytes 3538948
  350.7 16.6 %collective-permute-start.14 = (bf16[4,384,384]{2,1,0:T(8,128)(2,1)S(1)}, bf16[4,384,384]{2,1,0:T(8,128)(2,1)S(1)}, u32[]{:S(2)}, u32[]{:S(2)}) collective-permute-start(bf16[4,384,384]{2,1,0:T(8,128)(2,1)S(1)} %pad_maximum_fusion.1.refs_2_), channel_id=1, source_target_pairs={{0,1},{1,0},{2,3},{3,2},{4,5},{5,4},{6,7},{7,6},{8,9},{9,8},{10,11... | collective-permute-start | bytes 3538952 | tf_op jit(solution)/shard_map/ppermute | solution.py:37
  (4 other events, 4.3 us)
Sparse Core Ops, SparseCore 0:
  9.4 132.6 all-gather.2
  255.2 77.4 all-gather.4
